TPU v7x, 256 devices: a whole 4x4x8 slice. The times are simulated.
256 devices in a mesh: dp: 8 (over z), space: 32 (over x, y, core).
Axes of the slice: x: 4, y: 4, z: 8, core: 2. Of those that a mesh axis runs over, the one named last changes fastest.
Arguments:
- voxels: bfloat16 [131072, 256], P(('dp', 'space')), may hold values from -6 to 6
- counts: int32 [512], P(('dp', 'space')), may hold values from 32 to 256
- partners: int32 [512, 3], P(('dp', 'space')), may hold values from 0 to 511, as said below
- gain_attn: float32 [256], replicated, may hold values from 0.5 to 1.5
- w_qkv: bfloat16 [256, 768], replicated, may hold values from -5 to 5
- w_out: bfloat16 [256, 256], replicated, may hold values from -0.375 to 0.375
- gain_mlp: float32 [256], replicated, may hold values from 0.5 to 1.5
- w_up: bfloat16 [256, 1024], replicated, may hold values from -0.375 to 0.375
- w_down: bfloat16 [1024, 256], replicated, may hold values from -0.1875 to 0.1875
- cotangent: bfloat16 [131072, 256], P(('dp', 'space')), may hold values from -6 to 6
Outputs:
- output: bfloat16 [131072, 256], P(('dp', 'space'))
- grad_voxels: float32 [131072, 256], P(('dp', 'space'))
- grad_qkv: float32 [256, 768], replicated
- grad_out: float32 [256, 256], replicated
- grad_up: float32 [256, 1024], replicated
- grad_down: float32 [1024, 256], replicated
- grad_gain_attn: float32 [256], replicated
- grad_gain_mlp: float32 [256], replicated
Inputs may be any that keep to these rules, and one draw needn't show every extreme that they name: `partners`: blocks are numbered so that each index of dp holds a contiguous range of 512 / 8 blocks. Row i lists blocks of the same range as block i, each within 2 blocks of i and never i itself.
All inputs are finite; a program needn't handle non-finite values.
Results may differ from a plain program's by a relative error of at most 0.024.
The roundings to bfloat16 on the way count: a program that leaves them out, or rounds other values in their place, can miss the bound.
Values may be sent and summed in bfloat16 or wider, within the bound.
No kernel may reach another device: no remote copies, remote signals or barrier semaphores. Data moves between devices by JAX's collectives and lax.ppermute only.
A program may use at most 128 MiB of HBM per device.

v0:
```python
import math

import jax
import jax.numpy as jnp
from jax import lax
from jax.experimental import pallas as pl
from jax.experimental.pallas import tpu as pltpu
from jax.sharding import Mesh, PartitionSpec as P

HEADS = 8
HEAD = 32
BS = 256
PART = 3
SPAN = 2
SLOTS = PART + 1
D = 256
FF = 1024
LANES = 128
EXTRA = 8
PIECE = 32
FAR = 128.0
SHARE = ("core", "pair", "chip")
SPACE = ("chip", "core")

epsilon = 1e-06
root_coef = math.sqrt(2.0 / math.pi)
F32 = jnp.float32
BF16 = jnp.bfloat16
SCORE = 1.0 / math.sqrt(HEAD)
SCORE2 = math.log2(math.e) / math.sqrt(HEAD)


def mm(a, b):
    return lax.dot_general(a, b, (((1,), (0,)), ((), ())), preferred_element_type=F32)


def mm_t(a, b):
    return lax.dot_general(a, b, (((1,), (1,)), ((), ())), preferred_element_type=F32)


def t_mm(a, b):
    return lax.dot_general(a, b, (((0,), (0,)), ((), ())), preferred_element_type=F32)


def put_rows(ref, at, per, vals):
    for i in range(vals.shape[0] // PIECE):
        r = at + i * PIECE
        ref[r // per, r % per : r % per + PIECE, :] = vals[i * PIECE : (i + 1) * PIECE, :]


def main_kernel(local_blocks, partners, counts, xa, lo, hi, gain_attn, w_qkv, w_out, gain_mlp, w_up, w_down, cot,
                output, grads, to_lo, to_hi, gn_own, gm_out,
                bias_s, normed_s, xhat_s, k_s, v_s, kt_s, vt_s, qbt_s, gbt_s, qb_s, gb_s,
                s_s, e_s, ds_s, ot_s, linv_s, del_s, dk_s, dv_s, dqt_s, gnm_s, mix_s, oacc_s):
    nb = local_blocks
    ext = nb + 2 * SPAN
    per = grads.shape[1] - EXTRA
    g_attn = gain_attn[...]
    g_mlp = gain_mlp[...]
    zero_tile = jnp.zeros((D, BS), BF16)
    place = lax.axis_index("far") * lax.axis_size("pair") + lax.axis_index("pair")
    for axis in SPACE:
        place = place * lax.axis_size(axis) + lax.axis_index(axis)
    base = place * nb - SPAN
    lane_head = lax.broadcasted_iota(jnp.int32, (1, D), 1) // HEAD
    row_id = lax.broadcasted_iota(jnp.int32, (BS, BS), 0)

    for blk in range(ext):
        if blk < SPAN:
            src, at = lo, blk
        elif blk < SPAN + nb:
            src, at = xa, blk - SPAN
        else:
            src, at = hi, blk - SPAN - nb
        x = src[at * BS : (at + 1) * BS, :].astype(F32)
        inv = lax.rsqrt(jnp.mean(x * x, axis=-1, keepdims=True) + epsilon)
        xhat = x * inv
        xhat_s[blk] = xhat
        normed = (xhat * g_attn).astype(BF16)
        normed_s[blk] = normed
        if SPAN <= blk < SPAN + nb:
            bias_s[blk] = jnp.where(row_id < counts[at], 0.0, -1e30)
        else:
            bias_s[blk] = jnp.where(x > FAR / 2, -1e30, 0.0)
        k = mm(normed, w_qkv[:, D : 2 * D])
        k_s[blk] = k.astype(BF16)
        kt_s[blk] = k.T.astype(BF16)
        v = mm(normed, w_qkv[:, 2 * D :])
        v_s[blk] = v.astype(BF16)
        vt_s[blk] = v.T.astype(BF16)
        if SPAN <= blk < SPAN + nb:
            q = mm(normed, w_qkv[:, :D])
            qt = q.T.astype(BF16)
            for h in range(HEADS):
                qb_s[at, h] = jnp.where(lane_head == h, q, 0.0).astype(BF16)
                qbt_s[at, h] = zero_tile
                gbt_s[at, h] = zero_tile
                qbt_s[at, h, h * HEAD : (h + 1) * HEAD, :] = qt[h * HEAD : (h + 1) * HEAD, :]
        dk_s[blk] = jnp.zeros((BS, D), F32)
        dv_s[blk] = jnp.zeros((BS, D), F32)

    def slots(b):
        return [b + SPAN] + [partners[b, j] - base for j in range(PART)]

    steps = [(b, h) for b in range(nb) for h in range(HEADS)]
    ids = [slots(b) for b in range(nb)]

    def group(x):
        return x.reshape(BS // 8, 8, BS)

    def score(t):
        b, h = steps[t]
        top = None
        for j in range(SLOTS):
            s = mm(k_s[ids[b][j]], qbt_s[b, h]) + bias_s[ids[b][j]]
            s_s[t % 2, j] = s
            m = jnp.max(group(s), axis=0)
            top = m if top is None else jnp.maximum(top, m)
        return jnp.max(top, axis=0, keepdims=True)

    def weigh(t, top):
        b, h = steps[t]
        total = None
        for j in range(SLOTS):
            e = jnp.exp2((s_s[t % 2, j] - top) * SCORE2)
            e_s[b, h, j] = e.astype(BF16)
            p = jnp.sum(group(e), axis=0)
            total = p if total is None else total + p
        return 1.0 / jnp.sum(total, axis=0, keepdims=True)

    def gather(t, linv):
        b, h = steps[t]
        hs = slice(h * HEAD, (h + 1) * HEAD)
        out = None
        for j in range(SLOTS):
            o = mm(vt_s[ids[b][j], hs, :], e_s[b, h, j])
            out = o if out is None else out + o
        linv_s[t] = linv
        ot_s[b, hs, :] = out * linv

    tops, linvs = {}, {}
    for t in range(len(steps) + 2):
        if t < len(steps):
            tops[t] = score(t)
        if 1 <= t <= len(steps):
            linvs[t - 1] = weigh(t - 1, tops.pop(t - 1))
        if t >= 2:
            gather(t - 2, linvs.pop(t - 2))

    for b in range(nb):
        att = ot_s[b].astype(BF16)
        x = xa[b * BS : (b + 1) * BS, :].astype(F32)
        mixed = x + t_mm(att, w_out[...])
        mix_s[b * BS : (b + 1) * BS, :] = mixed
    mixed = mix_s[...]
    inv_m = lax.rsqrt(jnp.mean(mixed * mixed, axis=-1, keepdims=True) + epsilon)
    nm = (mixed * inv_m * g_mlp).astype(BF16)
    ct = cot[...]
    at_up = 3 * D * D // LANES
    at_down = at_up + D * FF // LANES
    at_out = at_down + D * FF // LANES
    chunk = 256
    for c in range(FF // chunk):
        cs = slice(c * chunk, (c + 1) * chunk)
        pre = mm(nm, w_up[:, cs])
        sq = pre * pre
        tangent = jnp.tanh(root_coef * (pre + 0.044715 * sq * pre))
        half = 0.5 * (1.0 + tangent)
        hidden = (pre * half).astype(BF16)
        slope = half + 0.5 * pre * (1.0 - tangent * tangent) * root_coef * (
            1.0 + 3.0 * 0.044715 * sq
        )
        o = mm(hidden, w_down[cs, :])
        gp = (mm_t(ct, w_down[cs, :]) * slope).astype(BF16)
        g = mm_t(gp, w_up[:, cs])
        if c == 0:
            oacc_s[...] = o
            gnm_s[...] = g
        else:
            oacc_s[...] += o
            gnm_s[...] += g
        down = t_mm(hidden, ct).astype(BF16)
        up = t_mm(nm, gp).astype(BF16)
        for i in range(D // LANES):
            put_rows(grads, at_down + i * FF + c * chunk, per, down[:, i * LANES : (i + 1) * LANES])
        for i in range(chunk // LANES):
            put_rows(grads, at_up + (c * (chunk // LANES) + i) * D, per, up[:, i * LANES : (i + 1) * LANES])
    output[...] = (mixed + oacc_s[...]).astype(BF16)
    gnm = gnm_s[...]
    scaled = gnm * g_mlp
    gm = ct.astype(F32) + inv_m * (
        scaled - mixed * (inv_m * inv_m) * jnp.mean(scaled * mixed, axis=-1, keepdims=True)
    )
    gm_out[...] = gm
    gain_mlp_sum = jnp.sum(gnm * mixed * inv_m, axis=0, keepdims=True)
    gmb = gm.astype(BF16)
    out_sum = None
    for b in range(nb):
        g_b = gmb[b * BS : (b + 1) * BS, :]
        o = mm(ot_s[b].astype(BF16), g_b)
        out_sum = o if out_sum is None else out_sum + o
        gt = mm_t(w_out[...], g_b).astype(BF16).astype(F32)
        pieces = []
        for h in range(HEADS):
            hs = slice(h * HEAD, (h + 1) * HEAD)
            gh = (gt[hs, :] * linv_s[b * HEADS + h]).astype(BF16)
            gbt_s[b, h, hs, :] = gh
            gf = gh.astype(F32)
            pieces.append(gf)
            del_s[b * HEADS + h] = jnp.sum(gf * ot_s[b, hs, :], axis=0, keepdims=True)
        gq = jnp.concatenate(pieces, axis=0).T
        for h in range(HEADS):
            gb_s[b, h] = jnp.where(lane_head == h, gq, 0.0).astype(BF16)
    out_sum = out_sum.astype(BF16)
    for i in range(D // LANES):
        put_rows(grads, at_out + i * D, per, out_sum[:, i * LANES : (i + 1) * LANES])

    def score_grad(t):
        b, h = steps[t]
        for j in range(SLOTS):
            gw = mm(v_s[ids[b][j]], gbt_s[b, h])
            ds_s[b, h, j] = (e_s[b, h, j].astype(F32) * (gw - del_s[t])).astype(BF16)

    def query_grad(t):
        b, h = steps[t]
        hs = slice(h * HEAD, (h + 1) * HEAD)
        dq = None
        for j in range(SLOTS):
            q = mm(kt_s[ids[b][j], hs, :], ds_s[b, h, j])
            dq = q if dq is None else dq + q
        dqt_s[b, hs, :] = dq * SCORE

    for t in range(len(steps) + 1):
        if t < len(steps):
            score_grad(t)
        if t >= 1:
            query_grad(t - 1)

    for b in range(nb):
        for j in range(SLOTS):
            dv = None
            dk = None
            for h in range(HEADS):
                a = mm(e_s[b, h, j], gb_s[b, h])
                dv = a if dv is None else dv + a
            for h in range(HEADS):
                a = mm(ds_s[b, h, j], qb_s[b, h])
                dk = a if dk is None else dk + a
            dv_s[ids[b][j]] += dv
            dk_s[ids[b][j]] += dk

    wq = w_qkv[:, :D]
    wk = w_qkv[:, D : 2 * D]
    wv = w_qkv[:, 2 * D :]
    sums = [None, None, None]
    gain_sum = None
    for blk in range(ext):
        normed = normed_s[blk]
        dk = (dk_s[blk] * SCORE).astype(BF16)
        dv = dv_s[blk].astype(BF16)
        gn = mm_t(dk, wk) + mm_t(dv, wv)
        parts = [(1, dk), (2, dv)]
        if SPAN <= blk < SPAN + nb:
            dq = dqt_s[blk - SPAN].T.astype(BF16)
            gn = gn + mm_t(dq, wq)
            parts.append((0, dq))
            gn_own[(blk - SPAN) * BS : (blk - SPAN + 1) * BS, :] = gn
        elif blk < SPAN:
            to_lo[blk * BS : (blk + 1) * BS, :] = gn.astype(BF16)
        else:
            to_hi[(blk - SPAN - nb) * BS : (blk - SPAN - nb + 1) * BS, :] = gn.astype(BF16)
        for which, val in parts:
            a = t_mm(normed, val)
            sums[which] = a if sums[which] is None else sums[which] + a
        g = jnp.sum(gn * xhat_s[blk], axis=0, keepdims=True)
        gain_sum = g if gain_sum is None else gain_sum + g
    for which in range(3):
        s = sums[which].astype(BF16)
        for i in range(D // LANES):
            put_rows(grads, (which * (D // LANES) + i) * D, per, s[:, i * LANES : (i + 1) * LANES])
    for r in range(grads.shape[0]):
        grads[r, per:, :] = jnp.zeros((EXTRA, LANES), BF16)
    for i in range(D // LANES):
        ls = slice(i * LANES, (i + 1) * LANES)
        grads[i, per:, :] = jnp.broadcast_to(gain_sum[:, ls], (EXTRA, LANES)).astype(BF16)
        grads[D // LANES + i, per:, :] = jnp.broadcast_to(gain_mlp_sum[:, ls], (EXTRA, LANES)).astype(BF16)


def back_kernel(xa, gm, gn_own, from_lo, from_hi, gain_attn, grad_voxels):
    rows = gm.shape[0]
    x = xa[:rows, :].astype(F32)
    inv = lax.rsqrt(jnp.mean(x * x, axis=-1, keepdims=True) + epsilon)
    gn = gn_own[...] + from_lo[...].astype(F32) + from_hi[...].astype(F32)
    scaled = gn * gain_attn[...]
    grad_voxels[...] = gm[...] + inv * (
        scaled - x * (inv * inv) * jnp.mean(scaled * x, axis=-1, keepdims=True)
    )


def get_rows(halves, at, per, count):
    half = halves[0].shape[0]
    out = []
    for i in range(count // PIECE):
        r = at + i * PIECE
        share = r // per
        ref = halves[share // half]
        out.append(ref[share % half, r % per : r % per + PIECE, :].astype(F32))
    return jnp.concatenate(out, axis=0)


def unpack_kernel(factor, mine, theirs, grad_qkv, grad_out, grad_up, grad_down, grad_ga, grad_gm):
    per = mine.shape[1] - EXTRA
    at_up = 3 * D * D // LANES
    at_down = at_up + D * FF // LANES
    at_out = at_down + D * FF // LANES

    def unpack(halves):
        for i in range(3 * D // LANES):
            grad_qkv[:, i * LANES : (i + 1) * LANES] = get_rows(halves, i * D, per, D) * factor
        for i in range(FF // LANES):
            grad_up[:, i * LANES : (i + 1) * LANES] = get_rows(halves, at_up + i * D, per, D) * factor
        for i in range(D // LANES):
            ls = slice(i * LANES, (i + 1) * LANES)
            grad_down[:, ls] = get_rows(halves, at_down + i * FF, per, FF) * factor
            grad_out[:, ls] = get_rows(halves, at_out + i * D, per, D) * factor
            grad_ga[:, ls] = halves[0][i, per : per + 1, :].astype(F32) * factor
            grad_gm[:, ls] = halves[0][D // LANES + i, per : per + 1, :].astype(F32) * factor

    core = lax.axis_index("core")
    pl.when(core == 0)(lambda: unpack((mine, theirs)))
    pl.when(core != 0)(lambda: unpack((theirs, mine)))


def sum_kernel(arrived, spread):
    total = arrived[0].astype(F32)
    for i in range(1, arrived.shape[0]):
        total = total + arrived[i].astype(F32)
    total = total.astype(BF16)
    for i in range(spread.shape[0]):
        spread[i] = total


VM = pl.BlockSpec(memory_space=pltpu.VMEM)
SM = pl.BlockSpec(memory_space=pltpu.SMEM)
PARAMS = pltpu.CompilerParams(vmem_limit_bytes=60 * 1024 * 1024)


def sds(shape, dtype):
    return jax.ShapeDtypeStruct(shape, dtype)


def sum_spread(arrived, copies):
    return pl.pallas_call(
        sum_kernel,
        out_shape=sds((copies, *arrived.shape[1:]), BF16),
        in_specs=[VM],
        out_specs=VM,
        compiler_params=PARAMS,
        name="sum_spread",
    )(arrived)


def exchange(x, axis):
    return lax.all_to_all(x, axis, split_axis=0, concat_axis=0, tiled=True)


def body(voxels, counts, partners, gain_attn, w_qkv, w_out, gain_mlp, w_up, w_down, cotangent):
    nb = counts.shape[0]
    rows = voxels.shape[0]
    n_space = lax.axis_size(SPACE)
    n_share = lax.axis_size(SHARE)
    n_far = lax.axis_size("far")
    up = [(i, i + 1) for i in range(n_space - 1)]
    down = [(j, i) for i, j in up]
    held = lax.broadcasted_iota(jnp.int32, (nb, BS, D), 1) < counts[:, None, None]
    marked = jnp.where(held, voxels.reshape(nb, BS, D), jnp.asarray(FAR, BF16)).reshape(rows, D)
    lo = lax.ppermute(marked, SPACE, up)
    hi = lax.ppermute(marked, SPACE, down)
    ext = nb + 2 * SPAN
    per = (3 * D * D + D * D + 2 * D * FF) // LANES // n_share
    tile = (BS, D)
    scratch = [
        pltpu.VMEM((ext, *tile), F32),
        pltpu.VMEM((ext, *tile), BF16),
        pltpu.VMEM((ext, *tile), F32),
        pltpu.VMEM((ext, *tile), BF16),
        pltpu.VMEM((ext, *tile), BF16),
        pltpu.VMEM((ext, *tile), BF16),
        pltpu.VMEM((ext, *tile), BF16),
        pltpu.VMEM((nb, HEADS, *tile), BF16),
        pltpu.VMEM((nb, HEADS, *tile), BF16),
        pltpu.VMEM((nb, HEADS, *tile), BF16),
        pltpu.VMEM((nb, HEADS, *tile), BF16),
        pltpu.VMEM((2, SLOTS, BS, BS), F32),
        pltpu.VMEM((nb, HEADS, SLOTS, BS, BS), BF16),
        pltpu.VMEM((nb, HEADS, SLOTS, BS, BS), BF16),
        pltpu.VMEM((nb, *tile), F32),
        pltpu.VMEM((nb * HEADS, 1, BS), F32),
        pltpu.VMEM((nb * HEADS, 1, BS), F32),
        pltpu.VMEM((ext, *tile), F32),
        pltpu.VMEM((ext, *tile), F32),
        pltpu.VMEM((nb, *tile), F32),
        pltpu.VMEM((rows, D), F32),
        pltpu.VMEM((rows, D), F32),
        pltpu.VMEM((rows, D), F32),
    ]
    ga = gain_attn.reshape(1, D)
    gmlp = gain_mlp.reshape(1, D)
    output, grads, to_lo, to_hi, gn_own, gm = pl.pallas_call(
        lambda *refs: main_kernel(nb, *refs),
        out_shape=[
            sds((rows, D), BF16),
            sds((n_share, per + EXTRA, LANES), BF16),
            sds((rows, D), BF16),
            sds((rows, D), BF16),
            sds((rows, D), F32),
            sds((rows, D), F32),
        ],
        in_specs=[SM, SM] + [VM] * 10,
        out_specs=[VM] * 6,
        scratch_shapes=scratch,
        compiler_params=PARAMS,
        name="layer",
    )(partners, counts, voxels, lo, hi, ga, w_qkv, w_out, gmlp, w_up, w_down, cotangent)
    shares = exchange(grads, SHARE)
    spread = sum_spread(shares, n_far)
    to_lo, to_hi, spread = lax.optimization_barrier((to_lo, to_hi, spread))
    over_far = exchange(spread, "far")
    from_lo = lax.ppermute(to_hi, SPACE, up)
    from_hi = lax.ppermute(to_lo, SPACE, down)
    spread = sum_spread(over_far, n_share // 2)
    spread, from_lo, from_hi = lax.optimization_barrier((spread, from_lo, from_hi))
    mine = exchange(spread, ("pair", "chip"))
    grad_voxels = pl.pallas_call(
        back_kernel,
        out_shape=sds((rows, D), F32),
        in_specs=[VM] * 6,
        out_specs=VM,
        compiler_params=PARAMS,
        cost_estimate=pl.CostEstimate(flops=4000000, transcendentals=0, bytes_accessed=3000000),
        name="voxel_grad",
    )(voxels, gm, gn_own, from_lo, from_hi, ga)
    mine, grad_voxels = lax.optimization_barrier((mine, grad_voxels))
    theirs = lax.ppermute(mine, "core", [(0, 1), (1, 0)])
    factor = 1.0 / math.sqrt(rows * n_far * lax.axis_size("pair") * n_space)
    outs = pl.pallas_call(
        lambda *refs: unpack_kernel(factor, *refs),
        out_shape=[
            sds((D, 3 * D), F32),
            sds((D, D), F32),
            sds((D, FF), F32),
            sds((FF, D), F32),
            sds((1, D), F32),
            sds((1, D), F32),
        ],
        in_specs=[VM] * 2,
        out_specs=[VM] * 6,
        compiler_params=PARAMS,
        name="unpack",
    )(mine, theirs)
    grad_qkv, grad_out, grad_up, grad_down, grad_ga, grad_gm = outs
    return (output, grad_voxels, grad_qkv, grad_out, grad_up, grad_down, grad_ga.reshape(D), grad_gm.reshape(D))


def solution(mesh):
    n_dp, n_space = mesh.devices.shape
    fine = Mesh(mesh.devices.reshape(n_dp // 2, 2, n_space // 2, 2), ("far", "pair", "chip", "core"))
    row = ("far", "pair", "chip", "core")
    in_specs = (
        P(row, None),
        P(row),
        P(row, None),
        P(),
        P(),
        P(),
        P(),
        P(),
        P(),
        P(row, None),
    )
    out_specs = (P(row, None), P(row, None), P(), P(), P(), P(), P(), P())
    return jax.shard_map(body, mesh=fine, in_specs=in_specs, out_specs=out_specs, check_vma=False)
```

profile of v0, /device:TPU:1, one launch (start us, length us, event | category | flops | bytes accessed | tf_op | source)
XLA Modules:
  0.0 124.0 jit_solution(3113213416587271807)
XLA Ops:
  0.6 0.7 iota_compare_fusion
  1.4 1.1 broadcast_select_fusion
  2.5 5.1 %collective-permute-start.1 = (bf16[512,256]{1,0:T(8,128)(2,1)S(1)}, bf16[512,256]{1,0:T(8,128)(2,1)S(1)}, u32[]{:S(2)}, u32[]{:S(2)}) collective-permute-start(bf16[512,256]{1,0:T(8,128)(2,1)S(1)} %broadcast_select_fusion), channel_id=1, source_target_pairs={{1,0},{2,1},{3,2},{4,3},{5,4},{6,5},{7,6},{8,7},{9,8},{10,9},{11,1... | collective-permute-start | bytes 786440 | tf_op jit(solution)/shard_map/ppermute | solution.py:378
  7.6 1.9 %collective-permute-start = (bf16[512,256]{1,0:T(8,128)(2,1)S(1)}, bf16[512,256]{1,0:T(8,128)(2,1)S(1)}, u32[]{:S(2)}, u32[]{:S(2)}) collective-permute-start(bf16[512,256]{1,0:T(8,128)(2,1)S(1)} %broadcast_select_fusion), channel_id=1, source_target_pairs={{0,1},{1,2},{2,3},{3,4},{4,5},{5,6},{6,7},{7,8},{8,9},{9,10},{10,1... | collective-permute-start | bytes 786440 | tf_op jit(solution)/shard_map/ppermute | solution.py:377
  9.5 1.6 %collective-permute-done.1.refs_4_ = bf16[512,256]{1,0:T(8,128)(2,1)S(1)} collective-permute-done((bf16[512,256]{1,0:T(8,128)(2,1)S(1)}, bf16[512,256]{1,0:T(8,128)(2,1)S(1)}, u32[]{:S(2)}, u32[]{:S(2)}) %collective-permute-start.1) | collective-permute-done | bytes 262176 | tf_op jit(solution)/shard_map/ppermute | solution.py:378
  11.1 0.0 copy-start.4
  11.1 1.7 %collective-permute-done.refs_3_ = bf16[512,256]{1,0:T(8,128)(2,1)S(1)} collective-permute-done((bf16[512,256]{1,0:T(8,128)(2,1)S(1)}, bf16[512,256]{1,0:T(8,128)(2,1)S(1)}, u32[]{:S(2)}, u32[]{:S(2)}) %collective-permute-start) | collective-permute-done | bytes 262176 | tf_op jit(solution)/shard_map/ppermute | solution.py:377
  12.8 0.0 copy-start.5
  12.8 0.0 copy-done.4
  12.8 0.7 copy-done.5
  13.5 22.1 %layer.1 = (bf16[512,256]{1,0:T(8,128)(2,1)}, bf16[64,104,128]{2,1,0:T(8,128)(2,1)}, bf16[512,256]{1,0:T(8,128)(2,1)}, bf16[512,256]{1,0:T(8,128)(2,1)}, f32[512,256]{1,0:T(8,128)}, /*index=5*/f32[512,256]{1,0:T(8,128)}) custom-call(s32[2,3]{1,0:T(2,128)} %refs_0_.1, s32[2]{0:T(128)} %refs_1_.1, bf16[512,256]{1,0:T(8,128)(2,1)} %xa.1, ...), custom_call_target="tpu_custom_call" | custom-call | tf_op jit(solution)/shard_map/layer/pallas_call | solution.py:409
  35.6 36.3 %all_to_all.15.arrived = bf16[64,104,128]{2,1,0:T(8,128)(2,1)} all-to-all(bf16[64,104,128]{2,1,0:T(8,128)(2,1)} %get-tuple-element.31), channel_id=1, replica_groups=mesh['far'=4,'pair'=2,'chip'=16,'core'=2] {'core','pair','chip'}, dimensions={0} | all-to-all | bytes 3407872 | tf_op jit(solution)/shard_map/all_to_all | solution.py:364
  72.0 2.4 %sum_spread.2 = bf16[4,104,128]{2,1,0:T(8,128)(2,1)} custom-call(bf16[64,104,128]{2,1,0:T(8,128)(2,1)} %all_to_all.15.arrived), custom_call_target="tpu_custom_call" | custom-call | tf_op jit(solution)/shard_map/sum_spread/pallas_call | solution.py:353
  74.4 0.0 copy-done.7
  74.4 2.1 %collective-permute-start.2 = (bf16[512,256]{1,0:T(8,128)(2,1)S(1)}, bf16[512,256]{1,0:T(8,128)(2,1)S(1)}, u32[]{:S(2)}, u32[]{:S(2)}) collective-permute-start(bf16[512,256]{1,0:T(8,128)(2,1)S(1)} %copy-done.7), channel_id=1, source_target_pairs={{0,1},{1,2},{2,3},{3,4},{4,5},{5,6},{6,7},{7,8},{8,9},{9,10},{10,1... | collective-permute-start | bytes 786440 | tf_op jit(solution)/shard_map/ppermute | solution.py:429
  76.5 0.0 copy-done.6
  76.5 2.3 %collective-permute-start.3 = (bf16[512,256]{1,0:T(8,128)(2,1)S(1)}, bf16[512,256]{1,0:T(8,128)(2,1)S(1)}, u32[]{:S(2)}, u32[]{:S(2)}) collective-permute-start(bf16[512,256]{1,0:T(8,128)(2,1)S(1)} %copy-done.6), channel_id=1, source_target_pairs={{1,0},{2,1},{3,2},{4,3},{5,4},{6,5},{7,6},{8,7},{9,8},{10,9},{11,1... | collective-permute-start | bytes 786440 | tf_op jit(solution)/shard_map/ppermute | solution.py:430
  78.8 15.2 %all_to_all.16.arrived = bf16[4,104,128]{2,1,0:T(8,128)(2,1)} all-to-all(bf16[4,104,128]{2,1,0:T(8,128)(2,1)} %sum_spread.2), channel_id=1, replica_groups=mesh['far'=4,'pair'=2,'chip'=16,'core'=2] {'far'}, dimensions={0} | all-to-all | bytes 212992 | tf_op jit(solution)/shard_map/all_to_all | solution.py:364
  94.0 1.9 %sum_spread.3 = bf16[32,104,128]{2,1,0:T(8,128)(2,1)} custom-call(bf16[4,104,128]{2,1,0:T(8,128)(2,1)} %all_to_all.16.arrived), custom_call_target="tpu_custom_call" | custom-call | tf_op jit(solution)/shard_map/sum_spread/pallas_call | solution.py:353
  95.8 0.0 collective-permute-done.2.from_lo
  95.9 0.0 collective-permute-done.3.from_hi
  95.9 0.0 copy-start.3
  95.9 6.2 %all-to-all-start.2 = ((bf16[32,104,128]{2,1,0:T(8,128)(2,1)}), bf16[32,104,128]{2,1,0:T(8,128)(2,1)S(1)}, u32[]{:S(2)}, u32[]{:S(2)}) async-start(bf16[32,104,128]{2,1,0:T(8,128)(2,1)} %sum_spread.3), calls=%async_computation.2 | async-start | bytes 1703936 | tf_op jit(solution)/shard_map/all_to_all | solution.py:364
  102.1 0.0 copy-done.2
  102.1 0.0 copy-done.3
  102.1 2.5 %voxel_grad.1 = f32[512,256]{1,0:T(8,128)} custom-call(bf16[512,256]{1,0:T(8,128)(2,1)} %xa.1, f32[512,256]{1,0:T(8,128)} %get-tuple-element.36.gm, f32[512,256]{1,0:T(8,128)} %get-tuple-element.37.gn_own, bf16[512,256]{1,0:T(8,128)(2,1)} %copy-done.2, bf16[512,256]{1,0:T(8,128)(2,1)} %copy-done.3, f32[1,256]{1,0:T(1,128)} %bitcast.5), custom_call_target="tpu_custom_call" | custom-call | flops 4000000 | bytes 3000000 | tf_op jit(solution)/shard_map/voxel_grad/pallas_call | solution.py:434
  104.6 9.6 %all-to-all-done.2.refs_0_ = bf16[32,104,128]{2,1,0:T(8,128)(2,1)S(1)} async-done(((bf16[32,104,128]{2,1,0:T(8,128)(2,1)}), bf16[32,104,128]{2,1,0:T(8,128)(2,1)S(1)}, u32[]{:S(2)}, u32[]{:S(2)}) %all-to-all-start.2) | async-done | bytes 852000 | tf_op jit(solution)/shard_map/all_to_all | solution.py:364
  114.3 3.4 %collective-permute-start.4 = (bf16[32,104,128]{2,1,0:T(8,128)(2,1)S(1)}, bf16[32,104,128]{2,1,0:T(8,128)(2,1)S(1)}, u32[]{:S(2)}, u32[]{:S(2)}) collective-permute-start(bf16[32,104,128]{2,1,0:T(8,128)(2,1)S(1)} %all-to-all-done.2.refs_0_), channel_id=1, source_target_pairs={{0,1},{1,0},{2,3},{3,2},{4,5},{5,4},{6,7},{7,6},{8,9},{9,8},{10,11... | collective-permute-start | bytes 2555912 | tf_op jit(solution)/shard_map/ppermute | solution.py:444
  117.6 2.0 %collective-permute-done.4.refs_1_ = bf16[32,104,128]{2,1,0:T(8,128)(2,1)S(1)} collective-permute-done((bf16[32,104,128]{2,1,0:T(8,128)(2,1)S(1)}, bf16[32,104,128]{2,1,0:T(8,128)(2,1)S(1)}, u32[]{:S(2)}, u32[]{:S(2)}) %collective-permute-start.4) | collective-permute-done | bytes 852000 | tf_op jit(solution)/shard_map/ppermute | solution.py:444
  119.6 0.0 copy-done
  119.7 0.9 copy-done.1
  120.6 3.4 %unpack.1 = (f32[256,768]{1,0:T(8,128)}, f32[256,256]{1,0:T(8,128)}, f32[256,1024]{1,0:T(8,128)}, f32[1024,256]{1,0:T(8,128)}, f32[1,256]{1,0:T(1,128)}, /*index=5*/f32[1,256]{1,0:T(1,128)}) custom-call(bf16[32,104,128]{2,1,0:T(8,128)(2,1)} %copy-done, bf16[32,104,128]{2,1,0:T(8,128)(2,1)} %copy-done.1), custom_call_target="tpu_custom_call" | custom-call | tf_op jit(solution)/shard_map/unpack/pallas_call | solution.py:446
  (6 shorter events, 0.0 us)
Async XLA Ops:
  2.5 8.6 %collective-permute-start.1 = (bf16[512,256]{1,0:T(8,128)(2,1)S(1)}, bf16[512,256]{1,0:T(8,128)(2,1)S(1)}, u32[]{:S(2)}, u32[]{:S(2)}) collective-permute-start(bf16[512,256]{1,0:T(8,128)(2,1)S(1)} %broadcast_select_fusion), channel_id=1, source_target_pairs={{1,0},{2,1},{3,2},{4,3},{5,4},{6,5},{7,6},{8,7},{9,8},{10,9},{11,1... | collective-permute-start | bytes 786440 | tf_op jit(solution)/shard_map/ppermute | solution.py:378
  7.6 5.2 %collective-permute-start = (bf16[512,256]{1,0:T(8,128)(2,1)S(1)}, bf16[512,256]{1,0:T(8,128)(2,1)S(1)}, u32[]{:S(2)}, u32[]{:S(2)}) collective-permute-start(bf16[512,256]{1,0:T(8,128)(2,1)S(1)} %broadcast_select_fusion), channel_id=1, source_target_pairs={{0,1},{1,2},{2,3},{3,4},{4,5},{5,6},{6,7},{7,8},{8,9},{9,10},{10,1... | collective-permute-start | bytes 786440 | tf_op jit(solution)/shard_map/ppermute | solution.py:377
  11.1 1.7 %copy-start.4 = (bf16[512,256]{1,0:T(8,128)(2,1)}, bf16[512,256]{1,0:T(8,128)(2,1)S(1)}, u32[]{:S(2)}) copy-start(bf16[512,256]{1,0:T(8,128)(2,1)S(1)} %collective-permute-done.1.refs_4_) | copy-start | bytes 786436
  12.8 0.7 copy-start.5
  72.0 2.4 %copy-start.7 = (bf16[512,256]{1,0:T(8,128)(2,1)S(1)}, bf16[512,256]{1,0:T(8,128)(2,1)}, u32[]{:S(2)}) copy-start(bf16[512,256]{1,0:T(8,128)(2,1)} %get-tuple-element.33) | copy-start | bytes 786436
  72.0 4.5 %copy-start.6 = (bf16[512,256]{1,0:T(8,128)(2,1)S(1)}, bf16[512,256]{1,0:T(8,128)(2,1)}, u32[]{:S(2)}) copy-start(bf16[512,256]{1,0:T(8,128)(2,1)} %get-tuple-element.34) | copy-start | bytes 786436
  74.4 21.4 %collective-permute-start.2 = (bf16[512,256]{1,0:T(8,128)(2,1)S(1)}, bf16[512,256]{1,0:T(8,128)(2,1)S(1)}, u32[]{:S(2)}, u32[]{:S(2)}) collective-permute-start(bf16[512,256]{1,0:T(8,128)(2,1)S(1)} %copy-done.7), channel_id=1, source_target_pairs={{0,1},{1,2},{2,3},{3,4},{4,5},{5,6},{6,7},{7,8},{8,9},{9,10},{10,1... | collective-permute-start | bytes 786440 | tf_op jit(solution)/shard_map/ppermute | solution.py:429
  76.5 19.4 %collective-permute-start.3 = (bf16[512,256]{1,0:T(8,128)(2,1)S(1)}, bf16[512,256]{1,0:T(8,128)(2,1)S(1)}, u32[]{:S(2)}, u32[]{:S(2)}) collective-permute-start(bf16[512,256]{1,0:T(8,128)(2,1)S(1)} %copy-done.6), channel_id=1, source_target_pairs={{1,0},{2,1},{3,2},{4,3},{5,4},{6,5},{7,6},{8,7},{9,8},{10,9},{11,1... | collective-permute-start | bytes 786440 | tf_op jit(solution)/shard_map/ppermute | solution.py:430
  95.9 6.3 %copy-start.2 = (bf16[512,256]{1,0:T(8,128)(2,1)}, bf16[512,256]{1,0:T(8,128)(2,1)S(1)}, u32[]{:S(2)}) copy-start(bf16[512,256]{1,0:T(8,128)(2,1)S(1)} %collective-permute-done.2.from_lo) | copy-start | bytes 786436
  95.9 6.3 %copy-start.3 = (bf16[512,256]{1,0:T(8,128)(2,1)}, bf16[512,256]{1,0:T(8,128)(2,1)S(1)}, u32[]{:S(2)}) copy-start(bf16[512,256]{1,0:T(8,128)(2,1)S(1)} %collective-permute-done.3.from_hi) | copy-start | bytes 786436
  95.9 18.4 %all-to-all-start.2 = ((bf16[32,104,128]{2,1,0:T(8,128)(2,1)}), bf16[32,104,128]{2,1,0:T(8,128)(2,1)S(1)}, u32[]{:S(2)}, u32[]{:S(2)}) async-start(bf16[32,104,128]{2,1,0:T(8,128)(2,1)} %sum_spread.3), calls=%async_computation.2 | async-start | bytes 1703936 | tf_op jit(solution)/shard_map/all_to_all | solution.py:364
  114.3 5.4 %copy-start = (bf16[32,104,128]{2,1,0:T(8,128)(2,1)}, bf16[32,104,128]{2,1,0:T(8,128)(2,1)S(1)}, u32[]{:S(2)}) copy-start(bf16[32,104,128]{2,1,0:T(8,128)(2,1)S(1)} %all-to-all-done.2.refs_0_) | copy-start | bytes 2555908
  114.3 5.4 %collective-permute-start.4 = (bf16[32,104,128]{2,1,0:T(8,128)(2,1)S(1)}, bf16[32,104,128]{2,1,0:T(8,128)(2,1)S(1)}, u32[]{:S(2)}, u32[]{:S(2)}) collective-permute-start(bf16[32,104,128]{2,1,0:T(8,128)(2,1)S(1)} %all-to-all-done.2.refs_0_), channel_id=1, source_target_pairs={{0,1},{1,0},{2,3},{3,2},{4,5},{5,4},{6,7},{7,6},{8,9},{9,8},{10,11... | collective-permute-start | bytes 2555912 | tf_op jit(solution)/shard_map/ppermute | solution.py:444
  119.7 0.9 copy-start.1
where the time goes:
time: 125 us; the launch traced here: 124 us
  blocking collectives  51.6 us (41%)
  Pallas kernels  32.3 us (26%)
  starting transfers between devices  21 us (17%)
  waiting for transfers between devices  14.9 us (12%)
  other arithmetic  1.81 us (1%)
  local copies, waits for them, and re-layouts  1.68 us (1%)
    all_to_all x2, blocking collectives, exchange(): return lax.all_to_all(x, axis, split_axis=0, concat_axis=0, tiled=True)  51.6 us
    pallas_call x1, Pallas kernels, body(): pl.pallas_call(lambda *refs: main_kernel(nb, *refs), out_shape=[sds((rows...  22.1 us
    all_to_all x1, waiting for transfers between devices, exchange(): return lax.all_to_all(x, axis, split_axis=0, concat_axis=0, tiled=True)  9.64 us
    all_to_all x1, starting transfers between devices, exchange(): return lax.all_to_all(x, axis, split_axis=0, concat_axis=0, tiled=True)  6.23 us
    ppermute x1, starting transfers between devices, body(): hi = lax.ppermute(marked, SPACE, down)  5.11 us
    pallas_call x2, Pallas kernels, sum_spread(): pl.pallas_call(sum_kernel, out_shape=sds((copies, *arrived.shape[1:]), BF...  4.28 us
    pallas_call x1, Pallas kernels, body(): pl.pallas_call(lambda *refs: unpack_kernel(factor, *refs), out_shape=[sds...  3.37 us
    ppermute x1, starting transfers between devices, body(): theirs = lax.ppermute(mine, 'core', [(0, 1), (1, 0)])  3.37 us
  transfers between devices with their start and end apart: 6, of which 4 were waited for; matrix products, arithmetic and copies ran while one was open for 0% of the time, Pallas kernels for 4%

commit v1 on v0

--- a/solution.py
+++ b/solution.py
@@ -331,15 +331,6 @@
     pl.when(core != 0)(lambda: unpack((theirs, mine)))
 
 
-def sum_kernel(arrived, spread):
-    total = arrived[0].astype(F32)
-    for i in range(1, arrived.shape[0]):
-        total = total + arrived[i].astype(F32)
-    total = total.astype(BF16)
-    for i in range(spread.shape[0]):
-        spread[i] = total
-
-
 VM = pl.BlockSpec(memory_space=pltpu.VMEM)
 SM = pl.BlockSpec(memory_space=pltpu.SMEM)
 PARAMS = pltpu.CompilerParams(vmem_limit_bytes=60 * 1024 * 1024)
@@ -347,17 +338,6 @@
 
 def sds(shape, dtype):
     return jax.ShapeDtypeStruct(shape, dtype)
-
-
-def sum_spread(arrived, copies):
-    return pl.pallas_call(
-        sum_kernel,
-        out_shape=sds((copies, *arrived.shape[1:]), BF16),
-        in_specs=[VM],
-        out_specs=VM,
-        compiler_params=PARAMS,
-        name="sum_spread",
-    )(arrived)
 
 
 def exchange(x, axis):
@@ -423,14 +403,8 @@
         name="layer",
     )(partners, counts, voxels, lo, hi, ga, w_qkv, w_out, gmlp, w_up, w_down, cotangent)
     shares = exchange(grads, SHARE)
-    spread = sum_spread(shares, n_far)
-    to_lo, to_hi, spread = lax.optimization_barrier((to_lo, to_hi, spread))
-    over_far = exchange(spread, "far")
     from_lo = lax.ppermute(to_hi, SPACE, up)
     from_hi = lax.ppermute(to_lo, SPACE, down)
-    spread = sum_spread(over_far, n_share // 2)
-    spread, from_lo, from_hi = lax.optimization_barrier((spread, from_lo, from_hi))
-    mine = exchange(spread, ("pair", "chip"))
     grad_voxels = pl.pallas_call(
         back_kernel,
         out_shape=sds((rows, D), F32),
@@ -440,7 +414,16 @@
         cost_estimate=pl.CostEstimate(flops=4000000, transcendentals=0, bytes_accessed=3000000),
         name="voxel_grad",
     )(voxels, gm, gn_own, from_lo, from_hi, ga)
-    mine, grad_voxels = lax.optimization_barrier((mine, grad_voxels))
+    total = lax.optimization_barrier(jnp.sum(shares.astype(F32), axis=0))
+    total = lax.optimization_barrier(total.astype(BF16))
+    terms = [total.astype(F32)] + [
+        lax.ppermute(total, "far", [(i, i ^ k) for i in range(n_far)]).astype(F32)
+        for k in range(1, n_far)
+    ]
+    while len(terms) > 1:
+        terms = [terms[i] + terms[i + 1] for i in range(0, len(terms), 2)]
+    spread = jnp.broadcast_to(terms[0].astype(BF16), (n_share // 2, *total.shape))
+    mine = exchange(spread, ("pair", "chip"))
     theirs = lax.ppermute(mine, "core", [(0, 1), (1, 0)])
     factor = 1.0 / math.sqrt(rows * n_far * lax.axis_size("pair") * n_space)
     outs = pl.pallas_call(

time: 125 us -> 123 us (0.984)
  Pallas kernels: 32.3 us -> 28 us
  starting transfers between devices: 21 us -> 22.6 us
    all_to_all x1 -> x0, waiting for transfers between devices: 9.64 us -> none  [exchange(): return lax.all_to_all(x, axis, split_axis=0, concat_axis=0, tiled=True)]
    ppermute x0 -> x3, starting transfers between devices: none -> 7.39 us  [body(): lax.ppermute(total, 'far', [(i, i ^ k) for i in range(n_far)]).astype(F32)]
    all_to_all x1 -> x0, starting transfers between devices: 6.23 us -> none  [exchange(): return lax.all_to_all(x, axis, split_axis=0, concat_axis=0, tiled=True)]
    ppermute x0 -> x3, waiting for transfers between devices: none -> 4.84 us  [body(): lax.ppermute(total, 'far', [(i, i ^ k) for i in range(n_far)]).astype(F32)]
    ppermute x1, waiting for transfers between devices: 0.01 us -> 4.4 us  [body(): from_hi = lax.ppermute(to_lo, SPACE, down)]
    pallas_call x2 -> x0, Pallas kernels: 4.28 us -> none  [sum_spread(): pl.pallas_call(sum_kernel, out_shape=sds((copies, *arrived.shape[1:]), BF...]
    ppermute x1, waiting for transfers between devices: 2.01 us -> 0.01 us  [body(): theirs = lax.ppermute(mine, 'core', [(0, 1), (1, 0)])]
    ppermute x1, waiting for transfers between devices: 0.01 us -> 1.36 us  [body(): from_lo = lax.ppermute(to_hi, SPACE, up)]
  transfers between devices with their start and end apart: 6 -> 8, of which waited for: 4 -> 5; matrix products, arithmetic and copies ran while one was open for 0% -> 0% of each run, Pallas kernels for 4% -> 2%
where the time goes in v1:
time: 123 us; the launch traced here: 122 us
  blocking collectives  51.8 us (42%)
  Pallas kernels  28 us (23%)
  starting transfers between devices  22.6 us (18%)
  waiting for transfers between devices  13.9 us (11%)
  local copies, waits for them, and re-layouts  2.49 us (2%)
  other arithmetic  2.09 us (2%)
    all_to_all x2, blocking collectives, exchange(): return lax.all_to_all(x, axis, split_axis=0, concat_axis=0, tiled=True)  51.8 us
    pallas_call x1, Pallas kernels, body(): pl.pallas_call(lambda *refs: main_kernel(nb, *refs), out_shape=[sds((rows...  22.1 us
    ppermute x3, starting transfers between devices, body(): lax.ppermute(total, 'far', [(i, i ^ k) for i in range(n_far)]).astype(F32)  7.39 us
    ppermute x1, starting transfers between devices, body(): hi = lax.ppermute(marked, SPACE, down)  5.11 us
    ppermute x3, waiting for transfers between devices, body(): lax.ppermute(total, 'far', [(i, i ^ k) for i in range(n_far)]).astype(F32)  4.84 us
    ppermute x1, waiting for transfers between devices, body(): from_hi = lax.ppermute(to_lo, SPACE, down)  4.4 us
    ppermute x1, starting transfers between devices, body(): theirs = lax.ppermute(mine, 'core', [(0, 1), (1, 0)])  3.66 us
    pallas_call x1, Pallas kernels, body(): pl.pallas_call(lambda *refs: unpack_kernel(factor, *refs), out_shape=[sds...  3.37 us
  transfers between devices with their start and end apart: 8, of which 5 were waited for; matrix products, arithmetic and copies ran while one was open for 0% of the time, Pallas kernels for 2%

profile of v1, /device:TPU:1, one launch (start us, length us, event | category | flops | bytes accessed | tf_op | source)
XLA Modules:
  0.0 121.6 jit_solution(11092615747682070818)
XLA Ops:
  0.6 0.7 iota_compare_fusion
  1.4 1.1 broadcast_select_fusion
  2.5 5.1 %collective-permute-start.1 = (bf16[512,256]{1,0:T(8,128)(2,1)S(1)}, bf16[512,256]{1,0:T(8,128)(2,1)S(1)}, u32[]{:S(2)}, u32[]{:S(2)}) collective-permute-start(bf16[512,256]{1,0:T(8,128)(2,1)S(1)} %broadcast_select_fusion), channel_id=1, source_target_pairs={{1,0},{2,1},{3,2},{4,3},{5,4},{6,5},{7,6},{8,7},{9,8},{10,9},{11,1... | collective-permute-start | bytes 786440 | tf_op jit(solution)/shard_map/ppermute | solution.py:358
  7.6 1.9 %collective-permute-start = (bf16[512,256]{1,0:T(8,128)(2,1)S(1)}, bf16[512,256]{1,0:T(8,128)(2,1)S(1)}, u32[]{:S(2)}, u32[]{:S(2)}) collective-permute-start(bf16[512,256]{1,0:T(8,128)(2,1)S(1)} %broadcast_select_fusion), channel_id=1, source_target_pairs={{0,1},{1,2},{2,3},{3,4},{4,5},{5,6},{6,7},{7,8},{8,9},{9,10},{10,1... | collective-permute-start | bytes 786440 | tf_op jit(solution)/shard_map/ppermute | solution.py:357
  9.5 1.6 %collective-permute-done.1.refs_4_ = bf16[512,256]{1,0:T(8,128)(2,1)S(1)} collective-permute-done((bf16[512,256]{1,0:T(8,128)(2,1)S(1)}, bf16[512,256]{1,0:T(8,128)(2,1)S(1)}, u32[]{:S(2)}, u32[]{:S(2)}) %collective-permute-start.1) | collective-permute-done | bytes 262176 | tf_op jit(solution)/shard_map/ppermute | solution.py:358
  11.1 1.7 %collective-permute-done.refs_3_ = bf16[512,256]{1,0:T(8,128)(2,1)S(1)} collective-permute-done((bf16[512,256]{1,0:T(8,128)(2,1)S(1)}, bf16[512,256]{1,0:T(8,128)(2,1)S(1)}, u32[]{:S(2)}, u32[]{:S(2)}) %collective-permute-start) | collective-permute-done | bytes 262176 | tf_op jit(solution)/shard_map/ppermute | solution.py:357
  12.8 0.0 copy-done.2
  12.8 0.7 copy-done.3
  13.5 22.1 %layer.1 = (bf16[512,256]{1,0:T(8,128)(2,1)}, bf16[64,104,128]{2,1,0:T(8,128)(2,1)}, bf16[512,256]{1,0:T(8,128)(2,1)}, bf16[512,256]{1,0:T(8,128)(2,1)}, f32[512,256]{1,0:T(8,128)}, /*index=5*/f32[512,256]{1,0:T(8,128)}) custom-call(s32[2,3]{1,0:T(2,128)} %refs_0_.1, s32[2]{0:T(128)} %refs_1_.1, bf16[512,256]{1,0:T(8,128)(2,1)} %xa.1, ...), custom_call_target="tpu_custom_call" | custom-call | tf_op jit(solution)/shard_map/layer/pallas_call | solution.py:389
  35.6 36.2 %all_to_all.10 = bf16[64,104,128]{2,1,0:T(8,128)(2,1)S(1)} all-to-all(bf16[64,104,128]{2,1,0:T(8,128)(2,1)} %get-tuple-element.25), channel_id=1, replica_groups=mesh['far'=4,'pair'=2,'chip'=16,'core'=2] {'core','pair','chip'}, dimensions={0} | all-to-all | bytes 3407872 | tf_op jit(solution)/shard_map/all_to_all | solution.py:344
  71.9 0.3 convert_reduce_fusion
  72.1 0.0 copy-start.6
  72.1 5.2 %collective-permute-start.6 = (bf16[104,128]{1,0:T(8,128)(2,1)S(1)}, bf16[104,128]{1,0:T(8,128)(2,1)S(1)}, u32[]{:S(2)}, u32[]{:S(2)}) collective-permute-start(bf16[104,128]{1,0:T(8,128)(2,1)S(1)} %convert_reduce_fusion), channel_id=1, source_target_pairs={{0,192},{64,128},{128,64},{192,0},{1,193},{65,129},{129,65},{193,1... | collective-permute-start | bytes 79880 | tf_op jit(solution)/shard_map/ppermute | solution.py:420
  77.4 1.2 collective-permute-start.5
  78.5 1.0 collective-permute-start.4
  79.5 0.0 collective-permute-done.6
  79.5 4.8 %collective-permute-done.5 = bf16[104,128]{1,0:T(8,128)(2,1)S(1)} collective-permute-done((bf16[104,128]{1,0:T(8,128)(2,1)S(1)}, bf16[104,128]{1,0:T(8,128)(2,1)S(1)}, u32[]{:S(2)}, u32[]{:S(2)}) %collective-permute-start.5) | collective-permute-done | bytes 26656 | tf_op jit(solution)/shard_map/ppermute | solution.py:420
  84.4 0.0 collective-permute-done.4
  84.4 0.1 broadcast_in_dim.9
  84.5 15.5 %all_to_all.11.refs_0_ = bf16[32,104,128]{2,1,0:T(8,128)(2,1)S(1)} all-to-all(bf16[32,104,128]{2,1,0:T(8,128)(2,1)S(1)} %broadcast_in_dim.9), channel_id=1, replica_groups=mesh['far'=4,'pair'=2,'chip'=16,'core'=2] {'pair','chip'}, dimensions={0} | all-to-all | bytes 1703936 | tf_op jit(solution)/shard_map/all_to_all | solution.py:344
  100.1 3.7 %collective-permute-start.7 = (bf16[32,104,128]{2,1,0:T(8,128)(2,1)S(1)}, bf16[32,104,128]{2,1,0:T(8,128)(2,1)S(1)}, u32[]{:S(2)}, u32[]{:S(2)}) collective-permute-start(bf16[32,104,128]{2,1,0:T(8,128)(2,1)S(1)} %all_to_all.11.refs_0_), channel_id=1, source_target_pairs={{0,1},{1,0},{2,3},{3,2},{4,5},{5,4},{6,7},{7,6},{8,9},{9,8},{10,11... | collective-permute-start | bytes 2555912 | tf_op jit(solution)/shard_map/ppermute | solution.py:427
  103.7 0.0 copy-done.7
  103.7 2.6 %collective-permute-start.2 = (bf16[512,256]{1,0:T(8,128)(2,1)S(1)}, bf16[512,256]{1,0:T(8,128)(2,1)S(1)}, u32[]{:S(2)}, u32[]{:S(2)}) collective-permute-start(bf16[512,256]{1,0:T(8,128)(2,1)S(1)} %copy-done.7), channel_id=1, source_target_pairs={{0,1},{1,2},{2,3},{3,4},{4,5},{5,6},{6,7},{7,8},{8,9},{9,10},{10,1... | collective-permute-start | bytes 786440 | tf_op jit(solution)/shard_map/ppermute | solution.py:406
  106.4 0.0 copy-done.6
  106.4 1.9 %collective-permute-start.3 = (bf16[512,256]{1,0:T(8,128)(2,1)S(1)}, bf16[512,256]{1,0:T(8,128)(2,1)S(1)}, u32[]{:S(2)}, u32[]{:S(2)}) collective-permute-start(bf16[512,256]{1,0:T(8,128)(2,1)S(1)} %copy-done.6), channel_id=1, source_target_pairs={{1,0},{2,1},{3,2},{4,3},{5,4},{6,5},{7,6},{8,7},{9,8},{10,9},{11,1... | collective-permute-start | bytes 786440 | tf_op jit(solution)/shard_map/ppermute | solution.py:407
  108.3 1.4 %collective-permute-done.2.from_lo = bf16[512,256]{1,0:T(8,128)(2,1)S(1)} collective-permute-done((bf16[512,256]{1,0:T(8,128)(2,1)S(1)}, bf16[512,256]{1,0:T(8,128)(2,1)S(1)}, u32[]{:S(2)}, u32[]{:S(2)}) %collective-permute-start.2) | collective-permute-done | bytes 262176 | tf_op jit(solution)/shard_map/ppermute | solution.py:406
  109.7 4.4 %collective-permute-done.3.from_hi = bf16[512,256]{1,0:T(8,128)(2,1)S(1)} collective-permute-done((bf16[512,256]{1,0:T(8,128)(2,1)S(1)}, bf16[512,256]{1,0:T(8,128)(2,1)S(1)}, u32[]{:S(2)}, u32[]{:S(2)}) %collective-permute-start.3) | collective-permute-done | bytes 262176 | tf_op jit(solution)/shard_map/ppermute | solution.py:407
  114.1 0.7 copy-done.5
  114.8 2.5 %voxel_grad.1 = f32[512,256]{1,0:T(8,128)} custom-call(bf16[512,256]{1,0:T(8,128)(2,1)} %xa.1, f32[512,256]{1,0:T(8,128)} %get-tuple-element.21.gm, f32[512,256]{1,0:T(8,128)} %get-tuple-element.22.gn_own, bf16[512,256]{1,0:T(8,128)(2,1)} %copy-done.4, bf16[512,256]{1,0:T(8,128)(2,1)} %copy-done.5, f32[1,256]{1,0:T(1,128)} %bitcast.5), custom_call_target="tpu_custom_call" | custom-call | flops 4000000 | bytes 3000000 | tf_op jit(solution)/shard_map/voxel_grad/pallas_call | solution.py:408
  117.3 0.0 collective-permute-done.7.refs_1_
  117.3 0.9 copy-done.1
  118.2 3.4 %unpack.1 = (f32[256,768]{1,0:T(8,128)}, f32[256,256]{1,0:T(8,128)}, f32[256,1024]{1,0:T(8,128)}, f32[1024,256]{1,0:T(8,128)}, f32[1,256]{1,0:T(1,128)}, /*index=5*/f32[1,256]{1,0:T(1,128)}) custom-call(bf16[32,104,128]{2,1,0:T(8,128)(2,1)} %copy-done, bf16[32,104,128]{2,1,0:T(8,128)(2,1)} %copy-done.1), custom_call_target="tpu_custom_call" | custom-call | tf_op jit(solution)/shard_map/unpack/pallas_call | solution.py:429
  (11 shorter events, 0.1 us)
Async XLA Ops:
  2.5 8.6 %collective-permute-start.1 = (bf16[512,256]{1,0:T(8,128)(2,1)S(1)}, bf16[512,256]{1,0:T(8,128)(2,1)S(1)}, u32[]{:S(2)}, u32[]{:S(2)}) collective-permute-start(bf16[512,256]{1,0:T(8,128)(2,1)S(1)} %broadcast_select_fusion), channel_id=1, source_target_pairs={{1,0},{2,1},{3,2},{4,3},{5,4},{6,5},{7,6},{8,7},{9,8},{10,9},{11,1... | collective-permute-start | bytes 786440 | tf_op jit(solution)/shard_map/ppermute | solution.py:358
  7.6 5.2 %collective-permute-start = (bf16[512,256]{1,0:T(8,128)(2,1)S(1)}, bf16[512,256]{1,0:T(8,128)(2,1)S(1)}, u32[]{:S(2)}, u32[]{:S(2)}) collective-permute-start(bf16[512,256]{1,0:T(8,128)(2,1)S(1)} %broadcast_select_fusion), channel_id=1, source_target_pairs={{0,1},{1,2},{2,3},{3,4},{4,5},{5,6},{6,7},{7,8},{8,9},{9,10},{10,1... | collective-permute-start | bytes 786440 | tf_op jit(solution)/shard_map/ppermute | solution.py:357
  11.1 1.7 %copy-start.2 = (bf16[512,256]{1,0:T(8,128)(2,1)}, bf16[512,256]{1,0:T(8,128)(2,1)S(1)}, u32[]{:S(2)}) copy-start(bf16[512,256]{1,0:T(8,128)(2,1)S(1)} %collective-permute-done.1.refs_4_) | copy-start | bytes 786436
  12.8 0.7 copy-start.3
  72.1 31.6 %copy-start.7 = (bf16[512,256]{1,0:T(8,128)(2,1)S(1)}, bf16[512,256]{1,0:T(8,128)(2,1)}, u32[]{:S(2)}) copy-start(bf16[512,256]{1,0:T(8,128)(2,1)} %get-tuple-element.23) | copy-start | bytes 786436
  72.1 34.2 %copy-start.6 = (bf16[512,256]{1,0:T(8,128)(2,1)S(1)}, bf16[512,256]{1,0:T(8,128)(2,1)}, u32[]{:S(2)}) copy-start(bf16[512,256]{1,0:T(8,128)(2,1)} %get-tuple-element.24) | copy-start | bytes 786436
  72.1 7.4 %collective-permute-start.6 = (bf16[104,128]{1,0:T(8,128)(2,1)S(1)}, bf16[104,128]{1,0:T(8,128)(2,1)S(1)}, u32[]{:S(2)}, u32[]{:S(2)}) collective-permute-start(bf16[104,128]{1,0:T(8,128)(2,1)S(1)} %convert_reduce_fusion), channel_id=1, source_target_pairs={{0,192},{64,128},{128,64},{192,0},{1,193},{65,129},{129,65},{193,1... | collective-permute-start | bytes 79880 | tf_op jit(solution)/shard_map/ppermute | solution.py:420
  77.4 7.0 %collective-permute-start.5 = (bf16[104,128]{1,0:T(8,128)(2,1)S(1)}, bf16[104,128]{1,0:T(8,128)(2,1)S(1)}, u32[]{:S(2)}, u32[]{:S(2)}) collective-permute-start(bf16[104,128]{1,0:T(8,128)(2,1)S(1)} %convert_reduce_fusion), channel_id=1, source_target_pairs={{0,128},{64,192},{128,0},{192,64},{1,129},{65,193},{129,1},{193,65... | collective-permute-start | bytes 79880 | tf_op jit(solution)/shard_map/ppermute | solution.py:420
  78.5 5.9 %collective-permute-start.4 = (bf16[104,128]{1,0:T(8,128)(2,1)S(1)}, bf16[104,128]{1,0:T(8,128)(2,1)S(1)}, u32[]{:S(2)}, u32[]{:S(2)}) collective-permute-start(bf16[104,128]{1,0:T(8,128)(2,1)S(1)} %convert_reduce_fusion), channel_id=1, source_target_pairs={{0,64},{64,0},{128,192},{192,128},{1,65},{65,1},{129,193},{193,129... | collective-permute-start | bytes 79880 | tf_op jit(solution)/shard_map/ppermute | solution.py:420
  100.1 17.2 %copy-start = (bf16[32,104,128]{2,1,0:T(8,128)(2,1)}, bf16[32,104,128]{2,1,0:T(8,128)(2,1)S(1)}, u32[]{:S(2)}) copy-start(bf16[32,104,128]{2,1,0:T(8,128)(2,1)S(1)} %all_to_all.11.refs_0_) | copy-start | bytes 2555908
  100.1 17.2 %collective-permute-start.7 = (bf16[32,104,128]{2,1,0:T(8,128)(2,1)S(1)}, bf16[32,104,128]{2,1,0:T(8,128)(2,1)S(1)}, u32[]{:S(2)}, u32[]{:S(2)}) collective-permute-start(bf16[32,104,128]{2,1,0:T(8,128)(2,1)S(1)} %all_to_all.11.refs_0_), channel_id=1, source_target_pairs={{0,1},{1,0},{2,3},{3,2},{4,5},{5,4},{6,7},{7,6},{8,9},{9,8},{10,11... | collective-permute-start | bytes 2555912 | tf_op jit(solution)/shard_map/ppermute | solution.py:427
  103.7 5.9 %collective-permute-start.2 = (bf16[512,256]{1,0:T(8,128)(2,1)S(1)}, bf16[512,256]{1,0:T(8,128)(2,1)S(1)}, u32[]{:S(2)}, u32[]{:S(2)}) collective-permute-start(bf16[512,256]{1,0:T(8,128)(2,1)S(1)} %copy-done.7), channel_id=1, source_target_pairs={{0,1},{1,2},{2,3},{3,4},{4,5},{5,6},{6,7},{7,8},{8,9},{9,10},{10,1... | collective-permute-start | bytes 786440 | tf_op jit(solution)/shard_map/ppermute | solution.py:406
  106.4 7.7 %collective-permute-start.3 = (bf16[512,256]{1,0:T(8,128)(2,1)S(1)}, bf16[512,256]{1,0:T(8,128)(2,1)S(1)}, u32[]{:S(2)}, u32[]{:S(2)}) collective-permute-start(bf16[512,256]{1,0:T(8,128)(2,1)S(1)} %copy-done.6), channel_id=1, source_target_pairs={{1,0},{2,1},{3,2},{4,3},{5,4},{6,5},{7,6},{8,7},{9,8},{10,9},{11,1... | collective-permute-start | bytes 786440 | tf_op jit(solution)/shard_map/ppermute | solution.py:407
  109.7 4.4 %copy-start.4 = (bf16[512,256]{1,0:T(8,128)(2,1)}, bf16[512,256]{1,0:T(8,128)(2,1)S(1)}, u32[]{:S(2)}) copy-start(bf16[512,256]{1,0:T(8,128)(2,1)S(1)} %collective-permute-done.2.from_lo) | copy-start | bytes 786436
  114.1 0.7 copy-start.5
  117.3 0.9 copy-start.1

commit v2 on v1

--- a/solution.py
+++ b/solution.py
@@ -286,12 +286,11 @@
         grads[D // LANES + i, per:, :] = jnp.broadcast_to(gain_mlp_sum[:, ls], (EXTRA, LANES)).astype(BF16)
 
 
-def back_kernel(xa, gm, gn_own, from_lo, from_hi, gain_attn, grad_voxels):
-    rows = gm.shape[0]
-    x = xa[:rows, :].astype(F32)
+def back_kernel(xa, gm, scaled_own, from_lo, from_hi, gain_attn, grad_voxels):
+    x = xa[...].astype(F32)
     inv = lax.rsqrt(jnp.mean(x * x, axis=-1, keepdims=True) + epsilon)
-    gn = gn_own[...] + from_lo[...].astype(F32) + from_hi[...].astype(F32)
-    scaled = gn * gain_attn[...]
+    halo = from_lo[...].astype(F32) + from_hi[...].astype(F32)
+    scaled = scaled_own[...] + halo * gain_attn[...]
     grad_voxels[...] = gm[...] + inv * (
         scaled - x * (inv * inv) * jnp.mean(scaled * x, axis=-1, keepdims=True)
     )
@@ -402,18 +401,15 @@
         compiler_params=PARAMS,
         name="layer",
     )(partners, counts, voxels, lo, hi, ga, w_qkv, w_out, gmlp, w_up, w_down, cotangent)
-    shares = exchange(grads, SHARE)
+    core = lax.axis_index("core")
+    halves = grads.reshape(2, n_share // 2, *grads.shape[1:])
+    got = lax.ppermute(lax.dynamic_index_in_dim(halves, 1 - core, 0, False), "core", [(0, 1), (1, 0)])
+    kept = lax.dynamic_index_in_dim(halves, core, 0, False)
+    half = (kept.astype(F32) + got.astype(F32)).astype(BF16)
+    shares = exchange(half, ("pair", "chip"))
     from_lo = lax.ppermute(to_hi, SPACE, up)
     from_hi = lax.ppermute(to_lo, SPACE, down)
-    grad_voxels = pl.pallas_call(
-        back_kernel,
-        out_shape=sds((rows, D), F32),
-        in_specs=[VM] * 6,
-        out_specs=VM,
-        compiler_params=PARAMS,
-        cost_estimate=pl.CostEstimate(flops=4000000, transcendentals=0, bytes_accessed=3000000),
-        name="voxel_grad",
-    )(voxels, gm, gn_own, from_lo, from_hi, ga)
+    scaled_own = lax.optimization_barrier(gn_own * ga)
     total = lax.optimization_barrier(jnp.sum(shares.astype(F32), axis=0))
     total = lax.optimization_barrier(total.astype(BF16))
     terms = [total.astype(F32)] + [
@@ -425,6 +421,15 @@
     spread = jnp.broadcast_to(terms[0].astype(BF16), (n_share // 2, *total.shape))
     mine = exchange(spread, ("pair", "chip"))
     theirs = lax.ppermute(mine, "core", [(0, 1), (1, 0)])
+    grad_voxels = pl.pallas_call(
+        back_kernel,
+        out_shape=sds((rows, D), F32),
+        in_specs=[VM] * 6,
+        out_specs=VM,
+        compiler_params=PARAMS,
+        cost_estimate=pl.CostEstimate(flops=4000000, transcendentals=0, bytes_accessed=3000000),
+        name="voxel_grad",
+    )(voxels, gm, scaled_own, from_lo, from_hi, ga)
     factor = 1.0 / math.sqrt(rows * n_far * lax.axis_size("pair") * n_space)
     outs = pl.pallas_call(
         lambda *refs: unpack_kernel(factor, *refs),

time: 123 us -> 115 us (0.935)
  blocking collectives: 51.8 us -> 40 us
  local copies, waits for them, and re-layouts: 2.49 us -> 3.87 us
    all_to_all x2, blocking collectives: 51.8 us -> 40 us  [exchange(): return lax.all_to_all(x, axis, split_axis=0, concat_axis=0, tiled=True)]
    ppermute x0 -> x1, waiting for transfers between devices: none -> 2.37 us  [body(): lax.ppermute(lax.dynamic_index_in_dim(halves, 1 - core, 0, False), 'core'...]
    squeeze x0 -> x1, local copies, waits for them, and re-layouts: none -> 1.35 us  [body(): lax.dynamic_index_in_dim(halves, 1 - core, 0, False)]
  transfers between devices with their start and end apart: 8 -> 9, of which waited for: 5 -> 6; matrix products, arithmetic and copies ran while one was open for 0% -> 1% of each run, Pallas kernels for 2% -> 2%
where the time goes in v2:
time: 115 us; the launch traced here: 114 us
  blocking collectives  40 us (35%)
  Pallas kernels  28 us (24%)
  starting transfers between devices  23.6 us (21%)
  waiting for transfers between devices  15.1 us (13%)
  local copies, waits for them, and re-layouts  3.87 us (3%)
  other arithmetic  3.01 us (3%)
    all_to_all x2, blocking collectives, exchange(): return lax.all_to_all(x, axis, split_axis=0, concat_axis=0, tiled=True)  40 us
    pallas_call x1, Pallas kernels, body(): pl.pallas_call(lambda *refs: main_kernel(nb, *refs), out_shape=[sds((rows...  22.1 us
    ppermute x3, starting transfers between devices, body(): lax.ppermute(total, 'far', [(i, i ^ k) for i in range(n_far)]).astype(F32)  7.39 us
    ppermute x1, starting transfers between devices, body(): hi = lax.ppermute(marked, SPACE, down)  5.11 us
    ppermute x1, starting transfers between devices, body(): theirs = lax.ppermute(mine, 'core', [(0, 1), (1, 0)])  4.56 us
    ppermute x3, waiting for transfers between devices, body(): lax.ppermute(total, 'far', [(i, i ^ k) for i in range(n_far)]).astype(F32)  4.53 us
    ppermute x1, waiting for transfers between devices, body(): from_hi = lax.ppermute(to_lo, SPACE, down)  4.4 us
    pallas_call x1, Pallas kernels, body(): pl.pallas_call(lambda *refs: unpack_kernel(factor, *refs), out_shape=[sds...  3.37 us
  transfers between devices with their start and end apart: 9, of which 6 were waited for; matrix products, arithmetic and copies ran while one was open for 1% of the time, Pallas kernels for 2%

profile of v2, /device:TPU:1, one launch (start us, length us, event | category | flops | bytes accessed | tf_op | source)
XLA Modules:
  0.0 114.3 jit_solution(16498839780474972394)
XLA Ops:
  0.6 0.7 iota_compare_fusion
  1.4 1.1 broadcast_select_fusion
  2.5 5.1 %collective-permute-start.1 = (bf16[512,256]{1,0:T(8,128)(2,1)S(1)}, bf16[512,256]{1,0:T(8,128)(2,1)S(1)}, u32[]{:S(2)}, u32[]{:S(2)}) collective-permute-start(bf16[512,256]{1,0:T(8,128)(2,1)S(1)} %broadcast_select_fusion), channel_id=1, source_target_pairs={{1,0},{2,1},{3,2},{4,3},{5,4},{6,5},{7,6},{8,7},{9,8},{10,9},{11,1... | collective-permute-start | bytes 786440 | tf_op jit(solution)/shard_map/ppermute | solution.py:357
  7.6 1.9 %collective-permute-start = (bf16[512,256]{1,0:T(8,128)(2,1)S(1)}, bf16[512,256]{1,0:T(8,128)(2,1)S(1)}, u32[]{:S(2)}, u32[]{:S(2)}) collective-permute-start(bf16[512,256]{1,0:T(8,128)(2,1)S(1)} %broadcast_select_fusion), channel_id=1, source_target_pairs={{0,1},{1,2},{2,3},{3,4},{4,5},{5,6},{6,7},{7,8},{8,9},{9,10},{10,1... | collective-permute-start | bytes 786440 | tf_op jit(solution)/shard_map/ppermute | solution.py:356
  9.5 1.6 %collective-permute-done.1.refs_4_ = bf16[512,256]{1,0:T(8,128)(2,1)S(1)} collective-permute-done((bf16[512,256]{1,0:T(8,128)(2,1)S(1)}, bf16[512,256]{1,0:T(8,128)(2,1)S(1)}, u32[]{:S(2)}, u32[]{:S(2)}) %collective-permute-start.1) | collective-permute-done | bytes 262176 | tf_op jit(solution)/shard_map/ppermute | solution.py:357
  11.1 1.7 %collective-permute-done.refs_3_ = bf16[512,256]{1,0:T(8,128)(2,1)S(1)} collective-permute-done((bf16[512,256]{1,0:T(8,128)(2,1)S(1)}, bf16[512,256]{1,0:T(8,128)(2,1)S(1)}, u32[]{:S(2)}, u32[]{:S(2)}) %collective-permute-start) | collective-permute-done | bytes 262176 | tf_op jit(solution)/shard_map/ppermute | solution.py:356
  12.8 0.7 copy-done.5
  13.5 22.1 %layer.1 = (bf16[512,256]{1,0:T(8,128)(2,1)}, bf16[64,104,128]{2,1,0:T(8,128)(2,1)}, bf16[512,256]{1,0:T(8,128)(2,1)}, bf16[512,256]{1,0:T(8,128)(2,1)}, f32[512,256]{1,0:T(8,128)}, /*index=5*/f32[512,256]{1,0:T(8,128)}) custom-call(s32[2,3]{1,0:T(2,128)} %refs_0_.1, s32[2]{0:T(128)} %refs_1_.1, bf16[512,256]{1,0:T(8,128)(2,1)} %xa.1, ...), custom_call_target="tpu_custom_call" | custom-call | tf_op jit(solution)/shard_map/layer/pallas_call | solution.py:388
  35.6 1.4 %dynamic-slice_bitcast_fusion = bf16[32,104,128]{2,1,0:T(8,128)(2,1)S(1)} fusion(bf16[2,32,104,128]{3,2,1,0:T(8,128)(2,1)} %bitcast.10, s32[]{:T(128)S(6)} %select_n.14), kind=kLoop, calls=%fused_computation.3 | loop fusion | bytes 1703940 | tf_op jit(solution)/shard_map/jit(dynamic_index_in_dim)/squeeze | solution.py:406
  37.0 0.1 collective-permute-start.4
  37.1 2.4 %collective-permute-done.4 = bf16[32,104,128]{2,1,0:T(8,128)(2,1)S(1)} collective-permute-done((bf16[32,104,128]{2,1,0:T(8,128)(2,1)S(1)}, bf16[32,104,128]{2,1,0:T(8,128)(2,1)S(1)}, u32[]{:S(2)}, u32[]{:S(2)}) %collective-permute-start.4) | collective-permute-done | bytes 852000 | tf_op jit(solution)/shard_map/ppermute | solution.py:406
  39.5 0.2 fusion
  39.7 23.7 %all_to_all.10 = bf16[32,104,128]{2,1,0:T(8,128)(2,1)S(1)} all-to-all(bf16[32,104,128]{2,1,0:T(8,128)(2,1)S(1)} %fusion), channel_id=1, replica_groups=mesh['far'=4,'pair'=2,'chip'=16,'core'=2] {'pair','chip'}, dimensions={0} | all-to-all | bytes 1703936 | tf_op jit(solution)/shard_map/all_to_all | solution.py:343
  63.4 0.1 convert_reduce_fusion
  63.5 5.2 %collective-permute-start.7 = (bf16[104,128]{1,0:T(8,128)(2,1)S(1)}, bf16[104,128]{1,0:T(8,128)(2,1)S(1)}, u32[]{:S(2)}, u32[]{:S(2)}) collective-permute-start(bf16[104,128]{1,0:T(8,128)(2,1)S(1)} %convert_reduce_fusion), channel_id=1, source_target_pairs={{0,192},{64,128},{128,64},{192,0},{1,193},{65,129},{129,65},{193,1... | collective-permute-start | bytes 79880 | tf_op jit(solution)/shard_map/ppermute | solution.py:416
  68.7 1.2 %collective-permute-start.6 = (bf16[104,128]{1,0:T(8,128)(2,1)S(1)}, bf16[104,128]{1,0:T(8,128)(2,1)S(1)}, u32[]{:S(2)}, u32[]{:S(2)}) collective-permute-start(bf16[104,128]{1,0:T(8,128)(2,1)S(1)} %convert_reduce_fusion), channel_id=1, source_target_pairs={{0,128},{64,192},{128,0},{192,64},{1,129},{65,193},{129,1},{193,65... | collective-permute-start | bytes 79880 | tf_op jit(solution)/shard_map/ppermute | solution.py:416
  69.9 1.0 collective-permute-start.5
  70.9 0.0 collective-permute-done.7
  70.9 4.5 %collective-permute-done.6 = bf16[104,128]{1,0:T(8,128)(2,1)S(1)} collective-permute-done((bf16[104,128]{1,0:T(8,128)(2,1)S(1)}, bf16[104,128]{1,0:T(8,128)(2,1)S(1)}, u32[]{:S(2)}, u32[]{:S(2)}) %collective-permute-start.6) | collective-permute-done | bytes 26656 | tf_op jit(solution)/shard_map/ppermute | solution.py:416
  75.4 0.0 collective-permute-done.5
  75.4 0.1 broadcast_in_dim.9
  75.5 16.3 %all_to_all.11.refs_0_ = bf16[32,104,128]{2,1,0:T(8,128)(2,1)S(1)} all-to-all(bf16[32,104,128]{2,1,0:T(8,128)(2,1)S(1)} %broadcast_in_dim.9), channel_id=1, replica_groups=mesh['far'=4,'pair'=2,'chip'=16,'core'=2] {'pair','chip'}, dimensions={0} | all-to-all | bytes 1703936 | tf_op jit(solution)/shard_map/all_to_all | solution.py:343
  91.9 4.6 %collective-permute-start.8 = (bf16[32,104,128]{2,1,0:T(8,128)(2,1)S(1)}, bf16[32,104,128]{2,1,0:T(8,128)(2,1)S(1)}, u32[]{:S(2)}, u32[]{:S(2)}) collective-permute-start(bf16[32,104,128]{2,1,0:T(8,128)(2,1)S(1)} %all_to_all.11.refs_0_), channel_id=1, source_target_pairs={{0,1},{1,0},{2,3},{3,2},{4,5},{5,4},{6,7},{7,6},{8,9},{9,8},{10,11... | collective-permute-start | bytes 2555912 | tf_op jit(solution)/shard_map/ppermute | solution.py:423
  96.4 2.6 %collective-permute-start.2 = (bf16[512,256]{1,0:T(8,128)(2,1)S(1)}, bf16[512,256]{1,0:T(8,128)(2,1)S(1)}, u32[]{:S(2)}, u32[]{:S(2)}) collective-permute-start(bf16[512,256]{1,0:T(8,128)(2,1)S(1)} %copy-done.10), channel_id=1, source_target_pairs={{0,1},{1,2},{2,3},{3,4},{4,5},{5,6},{6,7},{7,8},{8,9},{9,10},{10,1... | collective-permute-start | bytes 786440 | tf_op jit(solution)/shard_map/ppermute | solution.py:410
  99.1 1.9 %collective-permute-start.3 = (bf16[512,256]{1,0:T(8,128)(2,1)S(1)}, bf16[512,256]{1,0:T(8,128)(2,1)S(1)}, u32[]{:S(2)}, u32[]{:S(2)}) collective-permute-start(bf16[512,256]{1,0:T(8,128)(2,1)S(1)} %copy-done.9), channel_id=1, source_target_pairs={{1,0},{2,1},{3,2},{4,3},{5,4},{6,5},{7,6},{8,7},{9,8},{10,9},{11,1... | collective-permute-start | bytes 786440 | tf_op jit(solution)/shard_map/ppermute | solution.py:411
  101.0 0.8 broadcast_multiply_fusion.scaled_own
  101.9 0.5 collective-permute-done.2.from_lo
  102.4 4.4 %collective-permute-done.3.from_hi = bf16[512,256]{1,0:T(8,128)(2,1)S(1)} collective-permute-done((bf16[512,256]{1,0:T(8,128)(2,1)S(1)}, bf16[512,256]{1,0:T(8,128)(2,1)S(1)}, u32[]{:S(2)}, u32[]{:S(2)}) %collective-permute-start.3) | collective-permute-done | bytes 262176 | tf_op jit(solution)/shard_map/ppermute | solution.py:411
  106.8 0.7 copy-done.7
  107.5 2.5 %voxel_grad.1 = f32[512,256]{1,0:T(8,128)} custom-call(bf16[512,256]{1,0:T(8,128)(2,1)} %xa.1, f32[512,256]{1,0:T(8,128)} %get-tuple-element.21.gm, f32[512,256]{1,0:T(8,128)} %broadcast_multiply_fusion.scaled_own, bf16[512,256]{1,0:T(8,128)(2,1)} %copy-done.6, bf16[512,256]{1,0:T(8,128)(2,1)} %copy-done.7, f32[1,256]{1,0:T(1,128)} %bitcast.13), custom_call_target="tpu_custom_call" | custom-call | flops 4000000 | bytes 3000000 | tf_op jit(solution)/shard_map/voxel_grad/pallas_call | solution.py:424
  110.0 1.0 copy-done.2
  110.9 3.4 %unpack.1 = (f32[256,768]{1,0:T(8,128)}, f32[256,256]{1,0:T(8,128)}, f32[256,1024]{1,0:T(8,128)}, f32[1024,256]{1,0:T(8,128)}, f32[1,256]{1,0:T(1,128)}, /*index=5*/f32[1,256]{1,0:T(1,128)}) custom-call(bf16[32,104,128]{2,1,0:T(8,128)(2,1)} %copy-done, bf16[32,104,128]{2,1,0:T(8,128)(2,1)} %copy-done.2), custom_call_target="tpu_custom_call" | custom-call | tf_op jit(solution)/shard_map/unpack/pallas_call | solution.py:434
  (22 shorter events, 0.1 us)
Async XLA Ops:
  2.5 8.6 %collective-permute-start.1 = (bf16[512,256]{1,0:T(8,128)(2,1)S(1)}, bf16[512,256]{1,0:T(8,128)(2,1)S(1)}, u32[]{:S(2)}, u32[]{:S(2)}) collective-permute-start(bf16[512,256]{1,0:T(8,128)(2,1)S(1)} %broadcast_select_fusion), channel_id=1, source_target_pairs={{1,0},{2,1},{3,2},{4,3},{5,4},{6,5},{7,6},{8,7},{9,8},{10,9},{11,1... | collective-permute-start | bytes 786440 | tf_op jit(solution)/shard_map/ppermute | solution.py:357
  7.6 5.2 %collective-permute-start = (bf16[512,256]{1,0:T(8,128)(2,1)S(1)}, bf16[512,256]{1,0:T(8,128)(2,1)S(1)}, u32[]{:S(2)}, u32[]{:S(2)}) collective-permute-start(bf16[512,256]{1,0:T(8,128)(2,1)S(1)} %broadcast_select_fusion), channel_id=1, source_target_pairs={{0,1},{1,2},{2,3},{3,4},{4,5},{5,6},{6,7},{7,8},{8,9},{9,10},{10,1... | collective-permute-start | bytes 786440 | tf_op jit(solution)/shard_map/ppermute | solution.py:356
  11.1 1.7 %copy-start.4 = (bf16[512,256]{1,0:T(8,128)(2,1)}, bf16[512,256]{1,0:T(8,128)(2,1)S(1)}, u32[]{:S(2)}) copy-start(bf16[512,256]{1,0:T(8,128)(2,1)S(1)} %collective-permute-done.1.refs_4_) | copy-start | bytes 786436
  12.8 0.7 copy-start.5
  35.6 3.8 %copy-start.1 = (bf16[64,104,128]{2,1,0:T(8,128)(2,1)S(1)}, bf16[64,104,128]{2,1,0:T(8,128)(2,1)}, u32[]{:S(2)}) copy-start(bf16[64,104,128]{2,1,0:T(8,128)(2,1)} %get-tuple-element.25) | copy-start | bytes 5111812
  37.0 2.5 %collective-permute-start.4 = (bf16[32,104,128]{2,1,0:T(8,128)(2,1)S(1)}, bf16[32,104,128]{2,1,0:T(8,128)(2,1)S(1)}, u32[]{:S(2)}, u32[]{:S(2)}) collective-permute-start(bf16[32,104,128]{2,1,0:T(8,128)(2,1)S(1)} %dynamic-slice_bitcast_fusion), channel_id=1, source_target_pairs={{0,1},{1,0},{2,3},{3,2},{4,5},{5,4},{6,7},{7,6},{8,9},{9,8},{10,11... | collective-permute-start | bytes 2555912 | tf_op jit(solution)/shard_map/ppermute | solution.py:406
  63.4 33.1 %copy-start.10 = (bf16[512,256]{1,0:T(8,128)(2,1)S(1)}, bf16[512,256]{1,0:T(8,128)(2,1)}, u32[]{:S(2)}) copy-start(bf16[512,256]{1,0:T(8,128)(2,1)} %get-tuple-element.23) | copy-start | bytes 786436
  63.4 35.7 %copy-start.9 = (bf16[512,256]{1,0:T(8,128)(2,1)S(1)}, bf16[512,256]{1,0:T(8,128)(2,1)}, u32[]{:S(2)}) copy-start(bf16[512,256]{1,0:T(8,128)(2,1)} %get-tuple-element.24) | copy-start | bytes 786436
  63.4 37.7 %copy-start.3 = (f32[512,256]{1,0:T(8,128)S(1)}, f32[512,256]{1,0:T(8,128)}, u32[]{:S(2)}) copy-start(f32[512,256]{1,0:T(8,128)} %get-tuple-element.22) | copy-start | bytes 1572868
  63.4 37.7 %copy-start.8 = (f32[256]{0:T(256)S(1)}, f32[256]{0:T(256)}, u32[]{:S(2)}) copy-start(f32[256]{0:T(256)} %param.13) | copy-start | bytes 3076
  63.5 7.4 %collective-permute-start.7 = (bf16[104,128]{1,0:T(8,128)(2,1)S(1)}, bf16[104,128]{1,0:T(8,128)(2,1)S(1)}, u32[]{:S(2)}, u32[]{:S(2)}) collective-permute-start(bf16[104,128]{1,0:T(8,128)(2,1)S(1)} %convert_reduce_fusion), channel_id=1, source_target_pairs={{0,192},{64,128},{128,64},{192,0},{1,193},{65,129},{129,65},{193,1... | collective-permute-start | bytes 79880 | tf_op jit(solution)/shard_map/ppermute | solution.py:416
  68.7 6.7 %collective-permute-start.6 = (bf16[104,128]{1,0:T(8,128)(2,1)S(1)}, bf16[104,128]{1,0:T(8,128)(2,1)S(1)}, u32[]{:S(2)}, u32[]{:S(2)}) collective-permute-start(bf16[104,128]{1,0:T(8,128)(2,1)S(1)} %convert_reduce_fusion), channel_id=1, source_target_pairs={{0,128},{64,192},{128,0},{192,64},{1,129},{65,193},{129,1},{193,65... | collective-permute-start | bytes 79880 | tf_op jit(solution)/shard_map/ppermute | solution.py:416
  69.9 5.5 %collective-permute-start.5 = (bf16[104,128]{1,0:T(8,128)(2,1)S(1)}, bf16[104,128]{1,0:T(8,128)(2,1)S(1)}, u32[]{:S(2)}, u32[]{:S(2)}) collective-permute-start(bf16[104,128]{1,0:T(8,128)(2,1)S(1)} %convert_reduce_fusion), channel_id=1, source_target_pairs={{0,64},{64,0},{128,192},{192,128},{1,65},{65,1},{129,193},{193,129... | collective-permute-start | bytes 79880 | tf_op jit(solution)/shard_map/ppermute | solution.py:416
  91.9 18.1 %copy-start = (bf16[32,104,128]{2,1,0:T(8,128)(2,1)}, bf16[32,104,128]{2,1,0:T(8,128)(2,1)S(1)}, u32[]{:S(2)}) copy-start(bf16[32,104,128]{2,1,0:T(8,128)(2,1)S(1)} %all_to_all.11.refs_0_) | copy-start | bytes 2555908
  91.9 18.1 %collective-permute-start.8 = (bf16[32,104,128]{2,1,0:T(8,128)(2,1)S(1)}, bf16[32,104,128]{2,1,0:T(8,128)(2,1)S(1)}, u32[]{:S(2)}, u32[]{:S(2)}) collective-permute-start(bf16[32,104,128]{2,1,0:T(8,128)(2,1)S(1)} %all_to_all.11.refs_0_), channel_id=1, source_target_pairs={{0,1},{1,0},{2,3},{3,2},{4,5},{5,4},{6,7},{7,6},{8,9},{9,8},{10,11... | collective-permute-start | bytes 2555912 | tf_op jit(solution)/shard_map/ppermute | solution.py:423
  96.4 5.9 %collective-permute-start.2 = (bf16[512,256]{1,0:T(8,128)(2,1)S(1)}, bf16[512,256]{1,0:T(8,128)(2,1)S(1)}, u32[]{:S(2)}, u32[]{:S(2)}) collective-permute-start(bf16[512,256]{1,0:T(8,128)(2,1)S(1)} %copy-done.10), channel_id=1, source_target_pairs={{0,1},{1,2},{2,3},{3,4},{4,5},{5,6},{6,7},{7,8},{8,9},{9,10},{10,1... | collective-permute-start | bytes 786440 | tf_op jit(solution)/shard_map/ppermute | solution.py:410
  99.1 7.7 %collective-permute-start.3 = (bf16[512,256]{1,0:T(8,128)(2,1)S(1)}, bf16[512,256]{1,0:T(8,128)(2,1)S(1)}, u32[]{:S(2)}, u32[]{:S(2)}) collective-permute-start(bf16[512,256]{1,0:T(8,128)(2,1)S(1)} %copy-done.9), channel_id=1, source_target_pairs={{1,0},{2,1},{3,2},{4,3},{5,4},{6,5},{7,6},{8,7},{9,8},{10,9},{11,1... | collective-permute-start | bytes 786440 | tf_op jit(solution)/shard_map/ppermute | solution.py:411
  102.4 4.4 %copy-start.6 = (bf16[512,256]{1,0:T(8,128)(2,1)}, bf16[512,256]{1,0:T(8,128)(2,1)S(1)}, u32[]{:S(2)}) copy-start(bf16[512,256]{1,0:T(8,128)(2,1)S(1)} %collective-permute-done.2.from_lo) | copy-start | bytes 786436
  106.8 0.7 copy-start.7
  110.0 1.0 copy-start.2

commit v3 on v2

--- a/solution.py
+++ b/solution.py
@@ -48,12 +48,20 @@
         ref[r // per, r % per : r % per + PIECE, :] = vals[i * PIECE : (i + 1) * PIECE, :]
 
 
-def main_kernel(local_blocks, partners, counts, xa, lo, hi, gain_attn, w_qkv, w_out, gain_mlp, w_up, w_down, cot,
-                output, grads, to_lo, to_hi, gn_own, gm_out,
+def main_kernel(local_blocks, partners, counts, xa, lo, hi, gain_attn, w_qkv, gain_mlp,
+                w_out_any, w_up_any, w_down_any, cot_any,
+                grads, to_lo, to_hi, gn_own, output_any, gm_any,
+                w_out, w_up, w_down, cot, output, gm_out, in_sems, out_sems,
                 bias_s, normed_s, xhat_s, k_s, v_s, kt_s, vt_s, qbt_s, gbt_s, qb_s, gb_s,
                 s_s, e_s, ds_s, ot_s, linv_s, del_s, dk_s, dv_s, dqt_s, gnm_s, mix_s, oacc_s):
     nb = local_blocks
     ext = nb + 2 * SPAN
+    late = [(w_out_any, w_out), (w_up_any, w_up), (w_down_any, w_down), (cot_any, cot)]
+    late = [pltpu.make_async_copy(*pair, in_sems.at[i]) for i, pair in enumerate(late)]
+    for copy in late:
+        copy.start()
+    early = [(output, output_any), (gm_out, gm_any)]
+    early = [pltpu.make_async_copy(*pair, out_sems.at[i]) for i, pair in enumerate(early)]
     per = grads.shape[1] - EXTRA
     g_attn = gain_attn[...]
     g_mlp = gain_mlp[...]
@@ -147,6 +155,8 @@
         if t >= 2:
             gather(t - 2, linvs.pop(t - 2))
 
+    for copy in late:
+        copy.wait()
     for b in range(nb):
         att = ot_s[b].astype(BF16)
         x = xa[b * BS : (b + 1) * BS, :].astype(F32)
@@ -186,12 +196,14 @@
         for i in range(chunk // LANES):
             put_rows(grads, at_up + (c * (chunk // LANES) + i) * D, per, up[:, i * LANES : (i + 1) * LANES])
     output[...] = (mixed + oacc_s[...]).astype(BF16)
+    early[0].start()
     gnm = gnm_s[...]
     scaled = gnm * g_mlp
     gm = ct.astype(F32) + inv_m * (
         scaled - mixed * (inv_m * inv_m) * jnp.mean(scaled * mixed, axis=-1, keepdims=True)
     )
     gm_out[...] = gm
+    early[1].start()
     gain_mlp_sum = jnp.sum(gnm * mixed * inv_m, axis=0, keepdims=True)
     gmb = gm.astype(BF16)
     out_sum = None
@@ -284,6 +296,8 @@
         ls = slice(i * LANES, (i + 1) * LANES)
         grads[i, per:, :] = jnp.broadcast_to(gain_sum[:, ls], (EXTRA, LANES)).astype(BF16)
         grads[D // LANES + i, per:, :] = jnp.broadcast_to(gain_mlp_sum[:, ls], (EXTRA, LANES)).astype(BF16)
+    for copy in early:
+        copy.wait()
 
 
 def back_kernel(xa, gm, scaled_own, from_lo, from_hi, gain_attn, grad_voxels):
@@ -307,31 +321,43 @@
     return jnp.concatenate(out, axis=0)
 
 
-def unpack_kernel(factor, mine, theirs, grad_qkv, grad_out, grad_up, grad_down, grad_ga, grad_gm):
+def unpack_kernel(factor, mine, theirs, *refs):
+    outs, bufs, sems = refs[:6], refs[6:12], refs[12]
+    grad_qkv, grad_out, grad_up, grad_down, grad_ga, grad_gm = bufs
     per = mine.shape[1] - EXTRA
     at_up = 3 * D * D // LANES
     at_down = at_up + D * FF // LANES
     at_out = at_down + D * FF // LANES
+    copies = [pltpu.make_async_copy(b, o, sems.at[i]) for i, (b, o) in enumerate(zip(bufs, outs))]
 
     def unpack(halves):
+        for i in range(FF // LANES):
+            grad_up[:, i * LANES : (i + 1) * LANES] = get_rows(halves, at_up + i * D, per, D) * factor
+        copies[2].start()
+        for i in range(D // LANES):
+            grad_down[:, i * LANES : (i + 1) * LANES] = get_rows(halves, at_down + i * FF, per, FF) * factor
+        copies[3].start()
         for i in range(3 * D // LANES):
             grad_qkv[:, i * LANES : (i + 1) * LANES] = get_rows(halves, i * D, per, D) * factor
-        for i in range(FF // LANES):
-            grad_up[:, i * LANES : (i + 1) * LANES] = get_rows(halves, at_up + i * D, per, D) * factor
+        copies[0].start()
         for i in range(D // LANES):
             ls = slice(i * LANES, (i + 1) * LANES)
-            grad_down[:, ls] = get_rows(halves, at_down + i * FF, per, FF) * factor
             grad_out[:, ls] = get_rows(halves, at_out + i * D, per, D) * factor
             grad_ga[:, ls] = halves[0][i, per : per + 1, :].astype(F32) * factor
             grad_gm[:, ls] = halves[0][D // LANES + i, per : per + 1, :].astype(F32) * factor
+        for i in (1, 4, 5):
+            copies[i].start()
 
     core = lax.axis_index("core")
     pl.when(core == 0)(lambda: unpack((mine, theirs)))
     pl.when(core != 0)(lambda: unpack((theirs, mine)))
+    for copy in copies:
+        copy.wait()
 
 
 VM = pl.BlockSpec(memory_space=pltpu.VMEM)
 SM = pl.BlockSpec(memory_space=pltpu.SMEM)
+ANY = pl.BlockSpec(memory_space=pl.ANY)
 PARAMS = pltpu.CompilerParams(vmem_limit_bytes=60 * 1024 * 1024)
 
 
@@ -385,22 +411,32 @@
     ]
     ga = gain_attn.reshape(1, D)
     gmlp = gain_mlp.reshape(1, D)
-    output, grads, to_lo, to_hi, gn_own, gm = pl.pallas_call(
+    own_copies = [
+        pltpu.VMEM(w_out.shape, BF16),
+        pltpu.VMEM(w_up.shape, BF16),
+        pltpu.VMEM(w_down.shape, BF16),
+        pltpu.VMEM((rows, D), BF16),
+        pltpu.VMEM((rows, D), BF16),
+        pltpu.VMEM((rows, D), F32),
+        pltpu.SemaphoreType.DMA((4,)),
+        pltpu.SemaphoreType.DMA((2,)),
+    ]
+    grads, to_lo, to_hi, gn_own, output, gm = pl.pallas_call(
         lambda *refs: main_kernel(nb, *refs),
         out_shape=[
-            sds((rows, D), BF16),
             sds((n_share, per + EXTRA, LANES), BF16),
             sds((rows, D), BF16),
             sds((rows, D), BF16),
             sds((rows, D), F32),
+            sds((rows, D), BF16),
             sds((rows, D), F32),
         ],
-        in_specs=[SM, SM] + [VM] * 10,
-        out_specs=[VM] * 6,
-        scratch_shapes=scratch,
+        in_specs=[SM, SM] + [VM] * 6 + [ANY] * 4,
+        out_specs=[VM] * 4 + [ANY] * 2,
+        scratch_shapes=own_copies + scratch,
         compiler_params=PARAMS,
         name="layer",
-    )(partners, counts, voxels, lo, hi, ga, w_qkv, w_out, gmlp, w_up, w_down, cotangent)
+    )(partners, counts, voxels, lo, hi, ga, w_qkv, gmlp, w_out, w_up, w_down, cotangent)
     core = lax.axis_index("core")
     halves = grads.reshape(2, n_share // 2, *grads.shape[1:])
     got = lax.ppermute(lax.dynamic_index_in_dim(halves, 1 - core, 0, False), "core", [(0, 1), (1, 0)])
@@ -412,10 +448,10 @@
     scaled_own = lax.optimization_barrier(gn_own * ga)
     total = lax.optimization_barrier(jnp.sum(shares.astype(F32), axis=0))
     total = lax.optimization_barrier(total.astype(BF16))
-    terms = [total.astype(F32)] + [
-        lax.ppermute(total, "far", [(i, i ^ k) for i in range(n_far)]).astype(F32)
-        for k in range(1, n_far)
+    terms = [total] + [
+        lax.ppermute(total, "far", [(i, i ^ k) for i in range(n_far)]) for k in range(1, n_far)
     ]
+    terms = [term.astype(F32) for term in terms]
     while len(terms) > 1:
         terms = [terms[i] + terms[i + 1] for i in range(0, len(terms), 2)]
     spread = jnp.broadcast_to(terms[0].astype(BF16), (n_share // 2, *total.shape))
@@ -431,18 +467,13 @@
         name="voxel_grad",
     )(voxels, gm, scaled_own, from_lo, from_hi, ga)
     factor = 1.0 / math.sqrt(rows * n_far * lax.axis_size("pair") * n_space)
+    shapes = [(D, 3 * D), (D, D), (D, FF), (FF, D), (1, D), (1, D)]
     outs = pl.pallas_call(
         lambda *refs: unpack_kernel(factor, *refs),
-        out_shape=[
-            sds((D, 3 * D), F32),
-            sds((D, D), F32),
-            sds((D, FF), F32),
-            sds((FF, D), F32),
-            sds((1, D), F32),
-            sds((1, D), F32),
-        ],
+        out_shape=[sds(shape, F32) for shape in shapes],
         in_specs=[VM] * 2,
-        out_specs=[VM] * 6,
+        out_specs=[ANY] * 6,
+        scratch_shapes=[pltpu.VMEM(shape, F32) for shape in shapes] + [pltpu.SemaphoreType.DMA((6,))],
         compiler_params=PARAMS,
         name="unpack",
     )(mine, theirs)

time: 115 us -> 117 us (1.017)
  Pallas kernels: 28 us -> 29.6 us
    pallas_call x1, Pallas kernels: 22.1 us -> 23.8 us  [body(): pl.pallas_call(lambda *refs: main_kernel(nb, *refs), out_shape=[sds((n_sh...]
where the time goes in v3:
time: 117 us; the launch traced here: 116 us
  blocking collectives  40 us (34%)
  Pallas kernels  29.6 us (25%)
  starting transfers between devices  23.6 us (20%)
  waiting for transfers between devices  15.1 us (13%)
  local copies, waits for them, and re-layouts  3.87 us (3%)
  other arithmetic  3.01 us (3%)
    all_to_all x2, blocking collectives, exchange(): return lax.all_to_all(x, axis, split_axis=0, concat_axis=0, tiled=True)  40 us
    pallas_call x1, Pallas kernels, body(): pl.pallas_call(lambda *refs: main_kernel(nb, *refs), out_shape=[sds((n_sh...  23.8 us
    ppermute x3, starting transfers between devices, body(): lax.ppermute(total, 'far', [(i, i ^ k) for i in range(n_far)])  7.39 us
    ppermute x1, starting transfers between devices, body(): hi = lax.ppermute(marked, SPACE, down)  5.11 us
    ppermute x1, starting transfers between devices, body(): theirs = lax.ppermute(mine, 'core', [(0, 1), (1, 0)])  4.56 us
    ppermute x3, waiting for transfers between devices, body(): lax.ppermute(total, 'far', [(i, i ^ k) for i in range(n_far)])  4.53 us
    ppermute x1, waiting for transfers between devices, body(): from_hi = lax.ppermute(to_lo, SPACE, down)  4.4 us
    pallas_call x1, Pallas kernels, body(): pl.pallas_call(lambda *refs: unpack_kernel(factor, *refs), out_shape=[sds...  3.25 us
  transfers between devices with their start and end apart: 9, of which 6 were waited for; matrix products, arithmetic and copies ran while one was open for 1% of the time, Pallas kernels for 2%

profile of v3, /device:TPU:1, one launch (start us, length us, event | category | flops | bytes accessed | tf_op | source)
XLA Modules:
  0.0 116.1 jit_solution(12612859455098678305)
XLA Ops:
  0.6 0.7 iota_compare_fusion
  1.4 1.1 broadcast_select_fusion
  2.5 5.1 %collective-permute-start.1 = (bf16[512,256]{1,0:T(8,128)(2,1)S(1)}, bf16[512,256]{1,0:T(8,128)(2,1)S(1)}, u32[]{:S(2)}, u32[]{:S(2)}) collective-permute-start(bf16[512,256]{1,0:T(8,128)(2,1)S(1)} %broadcast_select_fusion), channel_id=1, source_target_pairs={{1,0},{2,1},{3,2},{4,3},{5,4},{6,5},{7,6},{8,7},{9,8},{10,9},{11,1... | collective-permute-start | bytes 786440 | tf_op jit(solution)/shard_map/ppermute | solution.py:383
  7.6 1.9 %collective-permute-start = (bf16[512,256]{1,0:T(8,128)(2,1)S(1)}, bf16[512,256]{1,0:T(8,128)(2,1)S(1)}, u32[]{:S(2)}, u32[]{:S(2)}) collective-permute-start(bf16[512,256]{1,0:T(8,128)(2,1)S(1)} %broadcast_select_fusion), channel_id=1, source_target_pairs={{0,1},{1,2},{2,3},{3,4},{4,5},{5,6},{6,7},{7,8},{8,9},{9,10},{10,1... | collective-permute-start | bytes 786440 | tf_op jit(solution)/shard_map/ppermute | solution.py:382
  9.5 1.6 %collective-permute-done.1.refs_4_ = bf16[512,256]{1,0:T(8,128)(2,1)S(1)} collective-permute-done((bf16[512,256]{1,0:T(8,128)(2,1)S(1)}, bf16[512,256]{1,0:T(8,128)(2,1)S(1)}, u32[]{:S(2)}, u32[]{:S(2)}) %collective-permute-start.1) | collective-permute-done | bytes 262176 | tf_op jit(solution)/shard_map/ppermute | solution.py:383
  11.1 1.7 %collective-permute-done.refs_3_ = bf16[512,256]{1,0:T(8,128)(2,1)S(1)} collective-permute-done((bf16[512,256]{1,0:T(8,128)(2,1)S(1)}, bf16[512,256]{1,0:T(8,128)(2,1)S(1)}, u32[]{:S(2)}, u32[]{:S(2)}) %collective-permute-start) | collective-permute-done | bytes 262176 | tf_op jit(solution)/shard_map/ppermute | solution.py:382
  12.8 0.7 copy-done.5
  13.5 23.8 %layer.1 = (bf16[64,104,128]{2,1,0:T(8,128)(2,1)}, bf16[512,256]{1,0:T(8,128)(2,1)}, bf16[512,256]{1,0:T(8,128)(2,1)}, f32[512,256]{1,0:T(8,128)}, bf16[512,256]{1,0:T(8,128)(2,1)}, /*index=5*/f32[512,256]{1,0:T(8,128)}) custom-call(s32[2,3]{1,0:T(2,128)} %refs_0_.1, s32[2]{0:T(128)} %refs_1_.1, bf16[512,256]{1,0:T(8,128)(2,1)} %xa.1, ...), custom_call_target="tpu_custom_call" | custom-call | tf_op jit(solution)/shard_map/layer/pallas_call | solution.py:424
  37.4 1.3 %dynamic-slice_bitcast_fusion = bf16[32,104,128]{2,1,0:T(8,128)(2,1)S(1)} fusion(bf16[2,32,104,128]{3,2,1,0:T(8,128)(2,1)} %bitcast.10, s32[]{:T(128)S(6)} %select_n.14), kind=kLoop, calls=%fused_computation.3 | loop fusion | bytes 1703940 | tf_op jit(solution)/shard_map/jit(dynamic_index_in_dim)/squeeze | solution.py:442
  38.7 0.1 collective-permute-start.4
  38.8 2.4 %collective-permute-done.4 = bf16[32,104,128]{2,1,0:T(8,128)(2,1)S(1)} collective-permute-done((bf16[32,104,128]{2,1,0:T(8,128)(2,1)S(1)}, bf16[32,104,128]{2,1,0:T(8,128)(2,1)S(1)}, u32[]{:S(2)}, u32[]{:S(2)}) %collective-permute-start.4) | collective-permute-done | bytes 852000 | tf_op jit(solution)/shard_map/ppermute | solution.py:442
  41.2 0.2 fusion
  41.4 23.7 %all_to_all.10 = bf16[32,104,128]{2,1,0:T(8,128)(2,1)S(1)} all-to-all(bf16[32,104,128]{2,1,0:T(8,128)(2,1)S(1)} %fusion), channel_id=1, replica_groups=mesh['far'=4,'pair'=2,'chip'=16,'core'=2] {'pair','chip'}, dimensions={0} | all-to-all | bytes 1703936 | tf_op jit(solution)/shard_map/all_to_all | solution.py:369
  65.1 0.1 convert_reduce_fusion
  65.2 5.2 %collective-permute-start.7 = (bf16[104,128]{1,0:T(8,128)(2,1)S(1)}, bf16[104,128]{1,0:T(8,128)(2,1)S(1)}, u32[]{:S(2)}, u32[]{:S(2)}) collective-permute-start(bf16[104,128]{1,0:T(8,128)(2,1)S(1)} %convert_reduce_fusion), channel_id=1, source_target_pairs={{0,192},{64,128},{128,64},{192,0},{1,193},{65,129},{129,65},{193,1... | collective-permute-start | bytes 79880 | tf_op jit(solution)/shard_map/ppermute | solution.py:452
  70.4 1.2 collective-permute-start.6
  71.6 1.0 collective-permute-start.5
  72.6 0.0 collective-permute-done.7
  72.6 4.5 %collective-permute-done.6 = bf16[104,128]{1,0:T(8,128)(2,1)S(1)} collective-permute-done((bf16[104,128]{1,0:T(8,128)(2,1)S(1)}, bf16[104,128]{1,0:T(8,128)(2,1)S(1)}, u32[]{:S(2)}, u32[]{:S(2)}) %collective-permute-start.6) | collective-permute-done | bytes 26656 | tf_op jit(solution)/shard_map/ppermute | solution.py:452
  77.1 0.0 collective-permute-done.5
  77.1 0.1 broadcast_in_dim.9
  77.3 16.3 %all_to_all.11.refs_0_ = bf16[32,104,128]{2,1,0:T(8,128)(2,1)S(1)} all-to-all(bf16[32,104,128]{2,1,0:T(8,128)(2,1)S(1)} %broadcast_in_dim.9), channel_id=1, replica_groups=mesh['far'=4,'pair'=2,'chip'=16,'core'=2] {'pair','chip'}, dimensions={0} | all-to-all | bytes 1703936 | tf_op jit(solution)/shard_map/all_to_all | solution.py:369
  93.6 4.6 %collective-permute-start.8 = (bf16[32,104,128]{2,1,0:T(8,128)(2,1)S(1)}, bf16[32,104,128]{2,1,0:T(8,128)(2,1)S(1)}, u32[]{:S(2)}, u32[]{:S(2)}) collective-permute-start(bf16[32,104,128]{2,1,0:T(8,128)(2,1)S(1)} %all_to_all.11.refs_0_), channel_id=1, source_target_pairs={{0,1},{1,0},{2,3},{3,2},{4,5},{5,4},{6,7},{7,6},{8,9},{9,8},{10,11... | collective-permute-start | bytes 2555912 | tf_op jit(solution)/shard_map/ppermute | solution.py:459
  98.2 2.6 %collective-permute-start.2 = (bf16[512,256]{1,0:T(8,128)(2,1)S(1)}, bf16[512,256]{1,0:T(8,128)(2,1)S(1)}, u32[]{:S(2)}, u32[]{:S(2)}) collective-permute-start(bf16[512,256]{1,0:T(8,128)(2,1)S(1)} %copy-done.10), channel_id=1, source_target_pairs={{0,1},{1,2},{2,3},{3,4},{4,5},{5,6},{6,7},{7,8},{8,9},{9,10},{10,1... | collective-permute-start | bytes 786440 | tf_op jit(solution)/shard_map/ppermute | solution.py:446
  100.8 1.9 %collective-permute-start.3 = (bf16[512,256]{1,0:T(8,128)(2,1)S(1)}, bf16[512,256]{1,0:T(8,128)(2,1)S(1)}, u32[]{:S(2)}, u32[]{:S(2)}) collective-permute-start(bf16[512,256]{1,0:T(8,128)(2,1)S(1)} %copy-done.9), channel_id=1, source_target_pairs={{1,0},{2,1},{3,2},{4,3},{5,4},{6,5},{7,6},{8,7},{9,8},{10,9},{11,1... | collective-permute-start | bytes 786440 | tf_op jit(solution)/shard_map/ppermute | solution.py:447
  102.7 0.8 broadcast_multiply_fusion.scaled_own
  103.6 0.5 collective-permute-done.2.from_lo
  104.1 4.4 %collective-permute-done.3.from_hi = bf16[512,256]{1,0:T(8,128)(2,1)S(1)} collective-permute-done((bf16[512,256]{1,0:T(8,128)(2,1)S(1)}, bf16[512,256]{1,0:T(8,128)(2,1)S(1)}, u32[]{:S(2)}, u32[]{:S(2)}) %collective-permute-start.3) | collective-permute-done | bytes 262176 | tf_op jit(solution)/shard_map/ppermute | solution.py:447
  108.5 0.7 copy-done.7
  109.2 2.5 %voxel_grad.1 = f32[512,256]{1,0:T(8,128)} custom-call(bf16[512,256]{1,0:T(8,128)(2,1)} %xa.1, f32[512,256]{1,0:T(8,128)} %get-tuple-element.21.gm, f32[512,256]{1,0:T(8,128)} %broadcast_multiply_fusion.scaled_own, bf16[512,256]{1,0:T(8,128)(2,1)} %copy-done.6, bf16[512,256]{1,0:T(8,128)(2,1)} %copy-done.7, f32[1,256]{1,0:T(1,128)} %bitcast.13), custom_call_target="tpu_custom_call" | custom-call | flops 4000000 | bytes 3000000 | tf_op jit(solution)/shard_map/voxel_grad/pallas_call | solution.py:460
  111.7 1.0 copy-done.2
  112.7 3.3 %unpack.1 = (f32[256,768]{1,0:T(8,128)}, f32[256,256]{1,0:T(8,128)}, f32[256,1024]{1,0:T(8,128)}, f32[1024,256]{1,0:T(8,128)}, f32[1,256]{1,0:T(1,128)}, /*index=5*/f32[1,256]{1,0:T(1,128)}) custom-call(bf16[32,104,128]{2,1,0:T(8,128)(2,1)} %copy-done, bf16[32,104,128]{2,1,0:T(8,128)(2,1)} %copy-done.2), custom_call_target="tpu_custom_call" | custom-call | tf_op jit(solution)/shard_map/unpack/pallas_call | solution.py:471
  (22 shorter events, 0.1 us)
Async XLA Ops:
  2.5 8.6 %collective-permute-start.1 = (bf16[512,256]{1,0:T(8,128)(2,1)S(1)}, bf16[512,256]{1,0:T(8,128)(2,1)S(1)}, u32[]{:S(2)}, u32[]{:S(2)}) collective-permute-start(bf16[512,256]{1,0:T(8,128)(2,1)S(1)} %broadcast_select_fusion), channel_id=1, source_target_pairs={{1,0},{2,1},{3,2},{4,3},{5,4},{6,5},{7,6},{8,7},{9,8},{10,9},{11,1... | collective-permute-start | bytes 786440 | tf_op jit(solution)/shard_map/ppermute | solution.py:383
  7.6 5.2 %collective-permute-start = (bf16[512,256]{1,0:T(8,128)(2,1)S(1)}, bf16[512,256]{1,0:T(8,128)(2,1)S(1)}, u32[]{:S(2)}, u32[]{:S(2)}) collective-permute-start(bf16[512,256]{1,0:T(8,128)(2,1)S(1)} %broadcast_select_fusion), channel_id=1, source_target_pairs={{0,1},{1,2},{2,3},{3,4},{4,5},{5,6},{6,7},{7,8},{8,9},{9,10},{10,1... | collective-permute-start | bytes 786440 | tf_op jit(solution)/shard_map/ppermute | solution.py:382
  11.1 1.7 %copy-start.4 = (bf16[512,256]{1,0:T(8,128)(2,1)}, bf16[512,256]{1,0:T(8,128)(2,1)S(1)}, u32[]{:S(2)}) copy-start(bf16[512,256]{1,0:T(8,128)(2,1)S(1)} %collective-permute-done.1.refs_4_) | copy-start | bytes 786436
  12.8 0.7 copy-start.5
  37.3 3.8 %copy-start.1 = (bf16[64,104,128]{2,1,0:T(8,128)(2,1)S(1)}, bf16[64,104,128]{2,1,0:T(8,128)(2,1)}, u32[]{:S(2)}) copy-start(bf16[64,104,128]{2,1,0:T(8,128)(2,1)} %get-tuple-element.25) | copy-start | bytes 5111812
  38.7 2.5 %collective-permute-start.4 = (bf16[32,104,128]{2,1,0:T(8,128)(2,1)S(1)}, bf16[32,104,128]{2,1,0:T(8,128)(2,1)S(1)}, u32[]{:S(2)}, u32[]{:S(2)}) collective-permute-start(bf16[32,104,128]{2,1,0:T(8,128)(2,1)S(1)} %dynamic-slice_bitcast_fusion), channel_id=1, source_target_pairs={{0,1},{1,0},{2,3},{3,2},{4,5},{5,4},{6,7},{7,6},{8,9},{9,8},{10,11... | collective-permute-start | bytes 2555912 | tf_op jit(solution)/shard_map/ppermute | solution.py:442
  65.1 33.1 %copy-start.10 = (bf16[512,256]{1,0:T(8,128)(2,1)S(1)}, bf16[512,256]{1,0:T(8,128)(2,1)}, u32[]{:S(2)}) copy-start(bf16[512,256]{1,0:T(8,128)(2,1)} %get-tuple-element.23) | copy-start | bytes 786436
  65.1 35.7 %copy-start.9 = (bf16[512,256]{1,0:T(8,128)(2,1)S(1)}, bf16[512,256]{1,0:T(8,128)(2,1)}, u32[]{:S(2)}) copy-start(bf16[512,256]{1,0:T(8,128)(2,1)} %get-tuple-element.24) | copy-start | bytes 786436
  65.1 37.7 %copy-start.3 = (f32[512,256]{1,0:T(8,128)S(1)}, f32[512,256]{1,0:T(8,128)}, u32[]{:S(2)}) copy-start(f32[512,256]{1,0:T(8,128)} %get-tuple-element.22) | copy-start | bytes 1572868
  65.1 37.7 %copy-start.8 = (f32[256]{0:T(256)S(1)}, f32[256]{0:T(256)}, u32[]{:S(2)}) copy-start(f32[256]{0:T(256)} %param.13) | copy-start | bytes 3076
  65.2 7.4 %collective-permute-start.7 = (bf16[104,128]{1,0:T(8,128)(2,1)S(1)}, bf16[104,128]{1,0:T(8,128)(2,1)S(1)}, u32[]{:S(2)}, u32[]{:S(2)}) collective-permute-start(bf16[104,128]{1,0:T(8,128)(2,1)S(1)} %convert_reduce_fusion), channel_id=1, source_target_pairs={{0,192},{64,128},{128,64},{192,0},{1,193},{65,129},{129,65},{193,1... | collective-permute-start | bytes 79880 | tf_op jit(solution)/shard_map/ppermute | solution.py:452
  70.4 6.7 %collective-permute-start.6 = (bf16[104,128]{1,0:T(8,128)(2,1)S(1)}, bf16[104,128]{1,0:T(8,128)(2,1)S(1)}, u32[]{:S(2)}, u32[]{:S(2)}) collective-permute-start(bf16[104,128]{1,0:T(8,128)(2,1)S(1)} %convert_reduce_fusion), channel_id=1, source_target_pairs={{0,128},{64,192},{128,0},{192,64},{1,129},{65,193},{129,1},{193,65... | collective-permute-start | bytes 79880 | tf_op jit(solution)/shard_map/ppermute | solution.py:452
  71.6 5.6 %collective-permute-start.5 = (bf16[104,128]{1,0:T(8,128)(2,1)S(1)}, bf16[104,128]{1,0:T(8,128)(2,1)S(1)}, u32[]{:S(2)}, u32[]{:S(2)}) collective-permute-start(bf16[104,128]{1,0:T(8,128)(2,1)S(1)} %convert_reduce_fusion), channel_id=1, source_target_pairs={{0,64},{64,0},{128,192},{192,128},{1,65},{65,1},{129,193},{193,129... | collective-permute-start | bytes 79880 | tf_op jit(solution)/shard_map/ppermute | solution.py:452
  93.6 18.1 %copy-start = (bf16[32,104,128]{2,1,0:T(8,128)(2,1)}, bf16[32,104,128]{2,1,0:T(8,128)(2,1)S(1)}, u32[]{:S(2)}) copy-start(bf16[32,104,128]{2,1,0:T(8,128)(2,1)S(1)} %all_to_all.11.refs_0_) | copy-start | bytes 2555908
  93.6 18.1 %collective-permute-start.8 = (bf16[32,104,128]{2,1,0:T(8,128)(2,1)S(1)}, bf16[32,104,128]{2,1,0:T(8,128)(2,1)S(1)}, u32[]{:S(2)}, u32[]{:S(2)}) collective-permute-start(bf16[32,104,128]{2,1,0:T(8,128)(2,1)S(1)} %all_to_all.11.refs_0_), channel_id=1, source_target_pairs={{0,1},{1,0},{2,3},{3,2},{4,5},{5,4},{6,7},{7,6},{8,9},{9,8},{10,11... | collective-permute-start | bytes 2555912 | tf_op jit(solution)/shard_map/ppermute | solution.py:459
  98.2 5.9 %collective-permute-start.2 = (bf16[512,256]{1,0:T(8,128)(2,1)S(1)}, bf16[512,256]{1,0:T(8,128)(2,1)S(1)}, u32[]{:S(2)}, u32[]{:S(2)}) collective-permute-start(bf16[512,256]{1,0:T(8,128)(2,1)S(1)} %copy-done.10), channel_id=1, source_target_pairs={{0,1},{1,2},{2,3},{3,4},{4,5},{5,6},{6,7},{7,8},{8,9},{9,10},{10,1... | collective-permute-start | bytes 786440 | tf_op jit(solution)/shard_map/ppermute | solution.py:446
  100.8 7.7 %collective-permute-start.3 = (bf16[512,256]{1,0:T(8,128)(2,1)S(1)}, bf16[512,256]{1,0:T(8,128)(2,1)S(1)}, u32[]{:S(2)}, u32[]{:S(2)}) collective-permute-start(bf16[512,256]{1,0:T(8,128)(2,1)S(1)} %copy-done.9), channel_id=1, source_target_pairs={{1,0},{2,1},{3,2},{4,3},{5,4},{6,5},{7,6},{8,7},{9,8},{10,9},{11,1... | collective-permute-start | bytes 786440 | tf_op jit(solution)/shard_map/ppermute | solution.py:447
  104.1 4.4 %copy-start.6 = (bf16[512,256]{1,0:T(8,128)(2,1)}, bf16[512,256]{1,0:T(8,128)(2,1)S(1)}, u32[]{:S(2)}) copy-start(bf16[512,256]{1,0:T(8,128)(2,1)S(1)} %collective-permute-done.2.from_lo) | copy-start | bytes 786436
  108.5 0.7 copy-start.7
  111.7 1.0 copy-start.2
